TPU v7x, 32 devices: a whole 2x2x4 slice. The times are simulated.
32 devices in a mesh: batch: 16 (over z, y, core), seq: 2 (over x).
Axes of the slice: x: 2, y: 2, z: 4, core: 2. Of those that a mesh axis runs over, the one named last changes fastest.
Arguments:
- hidden_in: bfloat16 [16, 1024, 768], P('batch', 'seq'), may hold values from -6 to 6
- segment_ids: int32 [16, 1024], P('batch'), may hold values from 0 to 3, never falling along the last dimension, each value on 1 to 512 neighbouring positions
- qkv_weight: bfloat16 [768, 2304], replicated, may hold values from -0.3125 to 0.3125
- qv_bias: float32 [2, 768], replicated, may hold values from -5 to 5
- out_weight: bfloat16 [768, 768], replicated, may hold values from -0.4375 to 0.4375
- out_bias: float32 [768], replicated, may hold values from -3 to 3
- norm_gain: float32 [2, 768], replicated, may hold values from 0.5 to 1.5
- norm_shift: float32 [2, 768], replicated, may hold values from -3 to 3
- ffn_in_weight: bfloat16 [768, 3072], replicated, may hold values from -0.21875 to 0.21875
- ffn_in_bias: float32 [3072], replicated, may hold values from -3 to 3
- ffn_out_weight: bfloat16 [3072, 768], replicated, may hold values from -0.15625 to 0.15625
- ffn_out_bias: float32 [768], replicated, may hold values from -3 to 3
- out_grad: bfloat16 [16, 1024, 768], P('batch', 'seq'), may hold values from -6 to 6
Outputs:
- hidden_out: bfloat16 [16, 1024, 768], P('batch', 'seq')
- input_grad: bfloat16 [16, 1024, 768], P('batch', 'seq')
- grad_qkv_weight: float32 [768, 2304], replicated
- grad_qv_bias: float32 [2, 768], replicated
- grad_out_weight: float32 [768, 768], replicated
- grad_out_bias: float32 [768], replicated
- grad_norm_gain: float32 [2, 768], replicated
- grad_norm_shift: float32 [2, 768], replicated
- grad_ffn_in_weight: float32 [768, 3072], replicated
- grad_ffn_in_bias: float32 [3072], replicated
- grad_ffn_out_weight: float32 [3072, 768], replicated
- grad_ffn_out_bias: float32 [768], replicated
Inputs may be any that keep to these rules, and one draw needn't show every extreme that they name: `segment_ids`: within a row the segment numbers never fall; a token attends only to tokens of its own row that carry its own number.
All inputs are finite; a program needn't handle non-finite values.
Results may differ from a plain program's by a relative error of at most 0.03.
Values may be sent and summed in bfloat16 or wider, within the bound.
A program may use at most 256 MiB of HBM per device.

v0:
```python
import math

import jax
import jax.numpy as jnp
from jax import lax
from jax.sharding import PartitionSpec as P

HEAD_DIM = 64
LAYERS = 2


epsilon = 1e-05
gelu_scale = 0.7978845608028654
masked_value = -1e30


def layer_norm(inputs, gain_row, shift_row):
    row_mean = jnp.mean(inputs, axis=-1, keepdims=True)
    offset = inputs - row_mean
    spread = jnp.mean(offset * offset, axis=-1, keepdims=True)
    return offset * lax.rsqrt(spread + epsilon) * gain_row + shift_row


def gelu_tanh(inputs):
    return (
        0.5 * inputs * (1.0 + jnp.tanh(gelu_scale * (inputs + 0.044715 * inputs * inputs * inputs)))
    )


def token_sum(gradient):
    return jnp.sum(gradient.astype(jnp.float32), axis=(0, 1))


def layer_forward(hidden_state, same_segment, weights):
    (
        weight_qkv,
        bias_qv,
        weight_out,
        bias_out,
        norm_gains,
        norm_shifts,
        weight_in,
        bias_in,
        weight_down,
        bias_down,
    ) = weights
    row_count, local_count, model_width = hidden_state.shape
    head_count = model_width // HEAD_DIM
    score_scale = HEAD_DIM ** (-0.5)
    state_low = hidden_state.astype(jnp.bfloat16)
    packed = jnp.dot(state_low, weight_qkv, preferred_element_type=jnp.float32)
    queries = (packed[..., :model_width] + bias_qv[0]).astype(jnp.bfloat16)
    keys_local = packed[..., model_width : 2 * model_width].astype(jnp.bfloat16)
    values_local = (packed[..., 2 * model_width :] + bias_qv[1]).astype(jnp.bfloat16)
    keys_all, values_all = (
        lax.all_gather(keys_local, "seq", axis=1, tiled=True),
        lax.all_gather(values_local, "seq", axis=1, tiled=True),
    )
    queries = queries.reshape(row_count, local_count, head_count, HEAD_DIM)
    keys_all = keys_all.reshape(row_count, -1, head_count, HEAD_DIM)
    values_all = values_all.reshape(row_count, -1, head_count, HEAD_DIM)
    scores = (
        jnp.einsum("rqhd,rkhd->rhqk", queries, keys_all, preferred_element_type=jnp.float32)
        * score_scale
    )
    scores = jnp.where(same_segment, scores, masked_value)
    row_maximum = jnp.max(scores, axis=-1, keepdims=True)
    exponents = jnp.exp(scores - row_maximum)
    totals = jnp.sum(exponents, axis=-1, keepdims=True)
    log_total = row_maximum + jnp.log(totals)
    softmax_low = (exponents / totals).astype(jnp.bfloat16)
    attended = jnp.einsum(
        "rhqk,rkhd->rqhd", softmax_low, values_all, preferred_element_type=jnp.float32
    )
    attended = attended.reshape(row_count, local_count, model_width).astype(jnp.bfloat16)
    residual = (
        hidden_state + jnp.dot(attended, weight_out, preferred_element_type=jnp.float32) + bias_out
    )
    normalized = layer_norm(residual, norm_gains[0], norm_shifts[0])
    normalized_low = normalized.astype(jnp.bfloat16)
    ffn_inner = jnp.dot(normalized_low, weight_in, preferred_element_type=jnp.float32) + bias_in
    activation = gelu_tanh(ffn_inner).astype(jnp.bfloat16)
    residual_two = (
        normalized
        + jnp.dot(activation, weight_down, preferred_element_type=jnp.float32)
        + bias_down
    )
    result = layer_norm(residual_two, norm_gains[1], norm_shifts[1])
    layer_cache = (
        state_low,
        queries,
        keys_all,
        values_all,
        log_total,
        attended,
        residual,
        normalized_low,
        ffn_inner,
        activation,
        residual_two,
    )
    return (result, layer_cache)


def layer_backward(gradient, layer_cache, same_segment, weights):
    (
        weight_qkv,
        bias_qv,
        weight_out,
        bias_out,
        norm_gains,
        norm_shifts,
        weight_in,
        bias_in,
        weight_down,
        bias_down,
    ) = weights
    (
        state_low,
        queries,
        keys_all,
        values_all,
        log_total,
        attended,
        residual,
        normalized_low,
        ffn_inner,
        activation,
        residual_two,
    ) = layer_cache
    row_count, local_count, model_width = gradient.shape
    head_count = model_width // HEAD_DIM
    score_scale = HEAD_DIM ** (-0.5)
    unused, norm_back = jax.vjp(layer_norm, residual_two, norm_gains[1], norm_shifts[1])
    grad_residual_two, grad_gain_two, grad_shift_two = norm_back(gradient)
    grad_branch_two = grad_residual_two.astype(jnp.bfloat16)
    grad_bias_down = token_sum(grad_branch_two)
    grad_weight_down = jnp.einsum(
        "rlf,rld->fd", activation, grad_branch_two, preferred_element_type=jnp.float32
    )
    grad_activation = jnp.dot(grad_branch_two, weight_down.T, preferred_element_type=jnp.float32)
    unused, gelu_back = jax.vjp(gelu_tanh, ffn_inner)
    grad_inner = gelu_back(grad_activation)[0].astype(jnp.bfloat16)
    grad_bias_in = token_sum(grad_inner)
    grad_weight_in = jnp.einsum(
        "rld,rlf->df", normalized_low, grad_inner, preferred_element_type=jnp.float32
    )
    grad_normalized = grad_residual_two + jnp.dot(
        grad_inner, weight_in.T, preferred_element_type=jnp.float32
    )
    unused, norm_back_one = jax.vjp(layer_norm, residual, norm_gains[0], norm_shifts[0])
    grad_residual, grad_gain_one, grad_shift_one = norm_back_one(grad_normalized)
    grad_branch = grad_residual.astype(jnp.bfloat16)
    grad_bias_out = token_sum(grad_branch)
    grad_weight_out = jnp.einsum(
        "rld,rle->de", attended, grad_branch, preferred_element_type=jnp.float32
    )
    grad_attended = jnp.dot(grad_branch, weight_out.T, preferred_element_type=jnp.float32).astype(
        jnp.bfloat16
    )
    grad_attended = grad_attended.reshape(row_count, local_count, head_count, HEAD_DIM)
    scores = (
        jnp.einsum("rqhd,rkhd->rhqk", queries, keys_all, preferred_element_type=jnp.float32)
        * score_scale
    )
    scores = jnp.where(same_segment, scores, masked_value)
    softmax_full = jnp.exp(scores - log_total)
    grad_probs = jnp.einsum(
        "rqhd,rkhd->rhqk", grad_attended, values_all, preferred_element_type=jnp.float32
    )
    grad_scores = softmax_full * (
        grad_probs - jnp.sum(softmax_full * grad_probs, axis=-1, keepdims=True)
    )
    grad_scores = grad_scores.astype(jnp.bfloat16)
    grad_queries = (
        jnp.einsum("rhqk,rkhd->rqhd", grad_scores, keys_all, preferred_element_type=jnp.float32)
        * score_scale
    )
    grad_queries = grad_queries.reshape(row_count, local_count, model_width).astype(jnp.bfloat16)
    key_terms = (
        jnp.einsum("rhqk,rqhd->rkhd", grad_scores, queries, preferred_element_type=jnp.float32)
        * score_scale
    )
    value_terms = jnp.einsum(
        "rhqk,rqhd->rkhd",
        softmax_full.astype(jnp.bfloat16),
        grad_attended,
        preferred_element_type=jnp.float32,
    )
    grad_keys, grad_values = (
        lax.psum_scatter(
            key_terms.reshape(row_count, -1, model_width).astype(jnp.bfloat16),
            "seq",
            scatter_dimension=1,
            tiled=True,
        ).astype(jnp.float32),
        lax.psum_scatter(
            value_terms.reshape(row_count, -1, model_width).astype(jnp.bfloat16),
            "seq",
            scatter_dimension=1,
            tiled=True,
        ).astype(jnp.float32),
    )
    grad_packed = jnp.concatenate(
        [grad_queries, grad_keys.astype(jnp.bfloat16), grad_values.astype(jnp.bfloat16)], axis=-1
    )
    grad_weight_qkv = jnp.einsum(
        "rld,rle->de", state_low, grad_packed, preferred_element_type=jnp.float32
    )
    packed_sums = token_sum(grad_packed)
    grad_bias_qv = jnp.stack([packed_sums[:model_width], packed_sums[2 * model_width :]])
    grad_state = grad_residual + jnp.dot(
        grad_packed, weight_qkv.T, preferred_element_type=jnp.float32
    )
    gradients = (
        grad_weight_qkv,
        grad_bias_qv,
        grad_weight_out,
        grad_bias_out,
        jnp.stack([grad_gain_one, grad_gain_two]),
        jnp.stack([grad_shift_one, grad_shift_two]),
        grad_weight_in,
        grad_bias_in,
        grad_weight_down,
        grad_bias_down,
    )
    return (grad_state, gradients)


def share(gradients):
    flat = jnp.concatenate([gradient_piece.reshape(-1) for gradient_piece in gradients])
    device_count = lax.axis_size(("batch", "seq"))
    flat = flat.reshape(device_count, -1)
    return lax.psum_scatter(flat, ("batch", "seq"), scatter_dimension=0, tiled=True)


def unshare(shares, piece_shapes):
    whole = (
        lax.all_gather(shares.astype(jnp.bfloat16), ("batch", "seq"), axis=0, tiled=True)
        .astype(shares.dtype)
        .reshape(-1)
    )
    pieces = []
    offset = 0
    for piece_shape in piece_shapes:
        amount = math.prod(piece_shape)
        pieces.append(whole[offset : offset + amount].reshape(piece_shape))
        offset = offset + amount
    return pieces


def per_device(
    hidden_in,
    segment_ids,
    qkv_weight,
    qv_bias,
    out_weight,
    out_bias,
    norm_gain,
    norm_shift,
    ffn_in_weight,
    ffn_in_bias,
    ffn_out_weight,
    ffn_out_bias,
    out_grad,
):
    weights = (
        qkv_weight,
        qv_bias,
        out_weight,
        out_bias,
        norm_gain,
        norm_shift,
        ffn_in_weight,
        ffn_in_bias,
        ffn_out_weight,
        ffn_out_bias,
    )
    local_count = hidden_in.shape[1]
    position = lax.axis_index("seq") * local_count
    query_segments = lax.dynamic_slice_in_dim(segment_ids, position, local_count, 1)
    same_segment = (query_segments[:, :, None] == segment_ids[:, None, :])[:, None]
    hidden_state = hidden_in.astype(jnp.float32)
    layer_inputs = []
    layer_caches = []
    for layer_index in range(LAYERS):
        layer_inputs.append(hidden_state)
        hidden_state, layer_cache = layer_forward(hidden_state, same_segment, weights)
        layer_caches.append(layer_cache)
    hidden_out = hidden_state.astype(jnp.bfloat16)
    gradient = out_grad.astype(jnp.float32)
    totals = None
    shares = None
    for layer_index in reversed(range(LAYERS)):
        layer_cache = layer_forward(layer_inputs[layer_index], same_segment, weights)[1]
        gradient, gradients = layer_backward(gradient, layer_cache, same_segment, weights)
        totals = (
            gradients
            if totals is None
            else tuple((first + second for first, second in zip(totals, gradients)))
        )
    shares = share(totals)
    pieces = unshare(shares, [weight_array.shape for weight_array in weights])
    input_grad = gradient.astype(jnp.bfloat16)
    return (
        hidden_out,
        input_grad,
        pieces[0],
        pieces[1],
        pieces[2],
        pieces[3],
        pieces[4],
        pieces[5],
        pieces[6],
        pieces[7],
        pieces[8],
        pieces[9],
    )


def solution(mesh):
    placed = (
        P("batch", "seq", None),
        P("batch", None),
        P(),
        P(),
        P(),
        P(),
        P(),
        P(),
        P(),
        P(),
        P(),
        P(),
        P("batch", "seq", None),
    )
    return jax.shard_map(
        per_device,
        mesh=mesh,
        in_specs=placed,
        out_specs=(
            P("batch", "seq", None),
            P("batch", "seq", None),
            P(),
            P(),
            P(),
            P(),
            P(),
            P(),
            P(),
            P(),
            P(),
            P(),
        ),
        check_vma=False,
    )
```

profile of v0, /device:TPU:0, one launch (start us, length us, event | category | flops | bytes accessed | tf_op | source)
XLA Modules:
  0.0 1787.7 jit_solution(17944282736636189084)
XLA Ops:
  9.2 3.1 convolution_bitcast_fusion.1
  16.2 3.3 fusion.45
  23.9 21.6 %all-gather.9.cloned.1.call-done = bf16[1,1024,768]{2,1,0:T(8,128)(2,1)} async-done(((bf16[1,512,768]{2,1,0:T(8,128)(2,1)}), bf16[1,1024,768]{2,1,0:T(8,128)(2,1)}) %all-gather.9.cloned.1.call-update) | async-done | bytes 1572880 | tf_op jit(solution)/shard_map/all_gather | solution.py:56
  45.6 2.7 copy.53
  48.3 14.8 fusion.12
  63.7 12.4 fusion
  76.1 2.6 copy.51
  78.7 12.1 fusion.57
  92.7 5.1 fusion.96
  97.9 4.2 fusion.113
  107.9 3.3 fusion.43
  113.5 21.9 %all-gather.13.cloned.1.call-done = bf16[1,1024,768]{2,1,0:T(8,128)(2,1)} async-done(((bf16[1,512,768]{2,1,0:T(8,128)(2,1)}), bf16[1,1024,768]{2,1,0:T(8,128)(2,1)}) %all-gather.13.cloned.1.call-update) | async-done | bytes 1572880 | tf_op jit(solution)/shard_map/all_gather | solution.py:56
  135.4 2.8 copy.56
  138.2 14.7 fusion.13
  153.0 11.8 fusion.1
  166.0 2.6 copy.54
  168.6 12.1 fusion.56
  182.3 5.8 fusion.102
  188.2 4.2 fusion.115
  196.4 8.2 convert_reduce_fusion.2
  204.6 3.7 multiply_reduce_fusion.4
  215.9 13.2 fusion.35
  229.2 18.9 %multiply_reduce_fusion.1 = (f32[12,512]{1,0:T(8,128)}, f32[12,512,1024]{2,1,0:T(8,128)}) fusion(f32[12,512]{1,0:T(8,128)} %log_add_fusion.1, f32[12,512,1024]{2,1,0:T(8,128)} %get-tuple-element.67, pred[512,1024]{1,0:T(8,128)(4,1)} %broadcast_compare_fusion, bf16[512,12,64]{0,2,1:T(8,128)(2,1)} %bitcast.214, bf16[1024,12,64]{0,2,1:T(8,128)(2,1)} %bitcast.209), kind=kOutput, calls=%fused_computation.5 | convolution fusion | flops 836757504 | bytes 53264384 | tf_op jit(solution)/shard_map/rqhd,rkhd->rhqk/dot_general | solution.py:168
  248.1 18.0 %multiply_convert_fusion.1 = bf16[12,512,1024]{2,1,0:T(8,128)(2,1)S(1)} fusion(f32[12,512,1024]{2,1,0:T(8,128)} %get-tuple-element.74, f32[12,512]{1,0:T(8,128)} %get-tuple-element.73, f32[12,512]{1,0:T(8,128)} %log_add_fusion.1, f32[12,512,1024]{2,1,0:T(8,128)} %get-tuple-element.67, pred[512,1024]{1,0:T(8,128)(4,1)} %broadcast_compare_fusion), kind=kLoop, calls=%fused_computation.4 | loop fusion | flops 37748736 | bytes 63488000 | tf_op jit(solution)/shard_map/convert_element_type | solution.py:174
  266.2 4.0 multiply_convert_fusion.5
  277.8 3.6 fusion.72
  281.4 9.7 fusion.100
  291.0 9.6 multiply_convert_fusion.7
  300.7 6.7 fusion.75
  307.4 6.0 multiply_reduce_fusion.2
  315.0 8.3 convert_reduce_fusion.1
  323.3 3.7 multiply_reduce_fusion.3
  334.6 13.2 fusion.38
  347.8 18.8 %multiply_reduce_fusion = (f32[12,512]{1,0:T(8,128)}, f32[12,512,1024]{2,1,0:T(8,128)}) fusion(f32[12,512]{1,0:T(8,128)} %log_add_fusion, f32[12,512,1024]{2,1,0:T(8,128)} %get-tuple-element.61, pred[512,1024]{1,0:T(8,128)(4,1)} %broadcast_compare_fusion, bf16[512,12,64]{0,2,1:T(8,128)(2,1)} %bitcast.216, bf16[1024,12,64]{0,2,1:T(8,128)(2,1)} %bitcast.207), kind=kOutput, calls=%fused_computation.2 | convolution fusion | flops 836757504 | bytes 53264384 | tf_op jit(solution)/shard_map/rqhd,rkhd->rhqk/dot_general | solution.py:168
  369.4 4.3 convolution_add_fusion.1
  374.9 17.1 multiply_convert_fusion
  392.1 4.1 multiply_convert_fusion.4
  401.0 3.4 reshape.945
  409.7 8.4 add_bitcast_fusion
  418.2 5.9 copy.61
  424.1 13.5 convolution_add_fusion
  437.6 11.1 reshape.947
  448.8 9.9 multiply_convert_fusion.6
  458.7 4.2 fusion.26
  462.9 5.3 bitcast_add_fusion
  468.3 7.9 reshape.944
  476.2 5.3 constant_dynamic-update-slice_fusion.5
  485.2 21.3 %dynamic-update-slice.2 = f32[7087104]{0:T(1024)} dynamic-update-slice(f32[7087104]{0:T(1024)} %constant_dynamic-update-slice_fusion.4, f32[589824]{0:T(1024)} %reshape.945, s32[]{} %constant.67) | dynamic-update-slice | bytes 4718596
  510.4 80.5 %dynamic-update-slice.6 = f32[7087104]{0:T(1024)} dynamic-update-slice(f32[7087104]{0:T(1024)} %constant_dynamic-update-slice_fusion.1, f32[2359296]{0:T(1024)} %bitcast.192, s32[]{} %constant.71) | dynamic-update-slice | bytes 18874372
  592.2 80.5 %dynamic-update-slice.8 = f32[7087104]{0:T(1024)} dynamic-update-slice(f32[7087104]{0:T(1024)} %add_dynamic-update-slice_fusion, f32[2359296]{0:T(1024)} %reshape.947, s32[]{} %constant.73) | dynamic-update-slice | bytes 18874372
  674.0 38.0 %reshape.948 = f32[32,221472]{1,0:T(8,128)} reshape(f32[7087104]{0:T(1024)} %constant_dynamic-update-slice_fusion) | data formatting | bytes 56696832 | tf_op jit(solution)/shard_map/reshape | solution.py:233
  712.1 456.8 %all-reduce.2 = bf16[32,221472]{1,0:T(8,128)(2,1)} all-reduce(f32[32,221472]{1,0:T(8,128)} %reshape.948), channel_id=6, replica_groups=mesh['batch'=16,'seq'=2] {'batch','seq'}, use_global_device_ids=true, to_apply=%region_42.43.clone | all-reduce | flops 7087104 | bytes 42522624
  1168.9 3.2 fusion.61
  1172.2 5.1 fusion.47
  1177.3 161.6 %all-gather.15.cloned.1.call-done = bf16[32,1,221472]{2,1,0:T(2,128)(2,1)} async-done(((bf16[1,1,221472]{2,1,0:T(2,128)(2,1)}), bf16[32,1,221472]{2,1,0:T(2,128)(2,1)}) %all-gather.15.cloned.1.call-update) | async-done | bytes 14174224 | tf_op jit(solution)/shard_map/all_gather | solution.py:239
  1338.9 303.2 %convert_reduce_fusion = f32[32,221472]{1,0:T(8,128)} fusion(bf16[32,1,221472]{2,1,0:T(2,128)(2,1)} %all-gather.15.cloned.1.call-done), kind=kLoop, calls=%fused_computation | loop fusion | flops 7087104 | bytes 42522624 | tf_op jit(solution)/shard_map/convert_element_type | solution.py:240
  1642.1 36.6 %reshape.966 = f32[7087104]{0:T(1024)} reshape(f32[32,221472]{1,0:T(8,128)} %convert_reduce_fusion) | data formatting | bytes 56696832
  1678.7 30.0 %slice.130 = f32[3076,2304]{1,0:T(8,128)} reshape(f32[7087104]{0:T(1024)} %reshape.966) | data formatting | bytes 56696832 | tf_op jit(solution)/shard_map/slice | solution.py:247
  1708.7 31.3 %slice.132 = f32[9228,768]{1,0:T(8,128)} reshape(f32[7087104]{0:T(1024)} %reshape.966) | data formatting | bytes 56696832 | tf_op jit(solution)/shard_map/slice | solution.py:247
  1741.4 3.2 slice.154
  1746.0 8.3 slice.158
  1755.6 8.0 slice.160
  1763.7 6.4 slice.152
  1770.1 10.9 reshape.950
  (324 shorter events, 80.0 us)
Async XLA Ops:
  7.2 8.4 copy-start.75
  7.2 38.4 %all-gather.9.cloned.1.call-start = ((), (), s32[]{:S(2)}) async-start(), calls=%async_computation.5 | async-start | bytes 2359296 | tf_op jit(solution)/shard_map/all_gather | solution.py:56
  14.5 7.4 copy-start.70
  15.5 60.6 %all-gather.7.cloned.1.call-start = ((), (), s32[]{:S(2)}) async-start(), calls=%async_computation.4 | async-start | bytes 2359296 | tf_op jit(solution)/shard_map/all_gather | solution.py:57
  19.5 116.0 %all-gather.13.cloned.1.call-start = ((), (), s32[]{:S(2)}) async-start(), calls=%async_computation.7 | async-start | bytes 2359296 | tf_op jit(solution)/shard_map/all_gather | solution.py:56
  23.9 170.1 %copy-start.43 = (f32[768]{0:T(1024)}, f32[768]{0:T(1024)S(1)}, u32[]{:S(2)}) copy-start(f32[768]{0:T(1024)S(1)} %get-tuple-element.26) | copy-start | bytes 9220
  48.3 15.4 copy-start.3
  78.7 12.1 copy-start.78
  78.7 12.1 copy-start.81
  78.7 12.1 copy-start.87
  90.8 7.0 copy-start.28
  90.8 7.0 slice-start
  107.8 58.2 %all-gather.11.cloned.1.call-start = ((), (), s32[]{:S(2)}) async-start(), calls=%async_computation.6 | async-start | bytes 2359296 | tf_op jit(solution)/shard_map/all_gather | solution.py:57
  113.5 193.9 %reduce-scatter.7.cloned.1.call-start = ((), (), s32[]{:S(2)}) async-start(), calls=%async_computation.9 | async-start | bytes 2359296 | tf_op jit(solution)/shard_map/reduce_scatter | solution.py:197
  138.2 14.8 copy-start.4
  153.0 11.8 copy-start.38
  168.6 12.1 copy-start.9
  168.6 12.1 copy-start.48
  168.6 12.2 copy-start.56
  168.6 12.2 copy-start.79
  168.6 12.2 copy-start.88
  180.7 7.4 copy-start.35
  180.8 7.3 slice-start.2
  181.9 26.4 %copy-start.16 = (f32[1,512,768]{2,1,0:T(8,128)}, f32[1,512,768]{2,1,0:T(8,128)S(1)}, u32[]{:S(2)}) copy-start(f32[1,512,768]{2,1,0:T(8,128)S(1)} %get-tuple-element.69) | copy-start | bytes 4718596
  181.9 26.4 %copy-start.59 = (f32[512]{0:T(512)}, f32[512]{0:T(512)S(1)}, u32[]{:S(2)}) copy-start(f32[512]{0:T(512)S(1)} %broadcast_multiply_fusion.1) | copy-start | bytes 6148
  182.2 26.1 %copy-start.71 = (f32[512]{0:T(512)}, f32[512]{0:T(512)S(1)}, u32[]{:S(2)}) copy-start(f32[512]{0:T(512)S(1)} %fusion.85) | copy-start | bytes 6148
  188.2 8.2 copy-start.92
  194.0 10.6 slice-start.6
  196.4 8.2 copy-start.33
  196.4 8.2 slice-start.7
  248.0 59.3 %reduce-scatter.5.cloned.1.call-start = ((), (), s32[]{:S(2)}) async-start(), calls=%async_computation.8 | async-start | bytes 2359296 | tf_op jit(solution)/shard_map/reduce_scatter | solution.py:191
  248.1 18.1 %copy-start.14 = (bf16[1,512,768]{1,2,0:T(8,128)(2,1)S(1)}, bf16[1,512,768]{1,2,0:T(8,128)(2,1)}, u32[]{:S(2)}) copy-start(bf16[1,512,768]{1,2,0:T(8,128)(2,1)} %copy.55) | copy-start | bytes 2359300
  271.2 10.1 copy-start.60
  271.2 187.4 %reduce-scatter.11.cloned.1.call-start = ((), (), s32[]{:S(2)}) async-start(), calls=%async_computation.11 | async-start | bytes 2359296 | tf_op jit(solution)/shard_map/reduce_scatter | solution.py:197
  281.4 9.7 copy-start.12
  281.4 19.3 %slice-start.12 = ((s8[6291456]{0:T(1024)(128)(4,1)}), s8[4194304]{0:T(1024)(128)(4,1)S(1)}, s32[]{:S(2)}) async-start(s8[6291456]{0:T(1024)(128)(4,1)} %bitcast.237), calls=%async_computation.25 | async-start | bytes 8388608
  291.0 9.6 copy-start.34
  291.0 9.6 copy-start.84
  291.0 9.6 slice-start.13
  300.7 6.7 copy-start.49
  307.4 7.6 slice-start.4
  307.4 7.6 slice-start.10
  307.4 7.5 slice-start.5
  307.4 7.5 slice-start.11
  313.4 9.8 slice-start.8
  314.9 8.3 copy-start.31
  314.9 8.3 copy-start.7
  315.0 8.3 copy-start.42
  315.0 8.3 copy-start.52
  315.0 8.3 slice-start.9
  366.6 92.0 %reduce-scatter.9.cloned.1.call-start = ((), (), s32[]{:S(2)}) async-start(), calls=%async_computation.10 | async-start | bytes 2359296 | tf_op jit(solution)/shard_map/reduce_scatter | solution.py:191
  366.7 7.0 copy-start.76
  366.7 7.6 copy-start.77
  366.7 8.2 copy-start.5
  366.7 8.2 copy-start.37
  366.7 8.2 copy-start.39
  374.9 17.1 copy-start.13
  397.2 941.7 %all-gather.15.cloned.1.call-start = ((), (), s32[]{:S(2)}) async-start(), calls=%async_computation.12 | async-start | bytes 29246976 | tf_op jit(solution)/shard_map/all_gather | solution.py:239
  481.5 26.2 %copy-start.53 = (f32[1536]{0:T(1024)S(1)}, f32[1536]{0:T(1024)}, u32[]{:S(2)}) copy-start(f32[1536]{0:T(1024)} %add.381) | copy-start | bytes 18436
  481.5 27.5 %copy-start.54 = (f32[1536]{0:T(1024)S(1)}, f32[1536]{0:T(1024)}, u32[]{:S(2)}) copy-start(f32[1536]{0:T(1024)} %add.383) | copy-start | bytes 18436
  510.4 80.5 %copy-start.69 = (f32[3072]{0:T(1024)S(1)}, f32[3072]{0:T(1024)}, u32[]{:S(2)}) copy-start(f32[3072]{0:T(1024)} %get-tuple-element.79) | copy-start | bytes 36868
  592.2 80.6 %copy-start.65 = (f32[768]{0:T(1024)S(1)}, f32[768]{0:T(1024)}, u32[]{:S(2)}) copy-start(f32[768]{0:T(1024)} %get-tuple-element.32) | copy-start | bytes 9220
  592.2 80.6 %copy-start.66 = (f32[768]{0:T(1024)S(1)}, f32[768]{0:T(1024)}, u32[]{:S(2)}) copy-start(f32[768]{0:T(1024)} %get-tuple-element.30) | copy-start | bytes 9220
  712.1 460.1 %copy-start.73 = (f32[512]{0:T(512)S(1)}, f32[512]{0:T(512)}, u32[]{:S(2)}) copy-start(f32[512]{0:T(512)} %copy-done.72) | copy-start | bytes 6148
  (53 other events, 203.3 us)
Sparse Core Ops, SparseCore 0:
  15.6 29.8 all-gather.8
  47.7 27.1 all-gather.6
  107.9 27.4 all-gather.12
  137.4 27.1 all-gather.10
  248.2 26.4 reduce-scatter.6
  276.7 26.1 reduce-scatter.4
  366.8 26.2 reduce-scatter.10
  397.3 26.2 reduce-scatter.8
  1172.3 166.5 all-gather.14
where the time goes:
time: 1810 us; the launch traced here: 1790 us
  blocking collectives  457 us (25%)
  local copies, waits for them, and re-layouts  453 us (25%)
  other arithmetic  391 us (22%)
  matrix products  266 us (15%)
  waiting for transfers between devices  205 us (11%)
    unnamed x1, blocking collectives  457 us
    convert_element_type x1, other arithmetic, unshare(): whole = lax.all_gather(shares.astype(jnp.bfloat16), ('batch', 'seq'), axi...  303 us
    unnamed x226, local copies, waits for them, and re-layouts  252 us
    all_gather x1, waiting for transfers between devices, unshare(): lax.all_gather(shares.astype(jnp.bfloat16), ('batch', 'seq'), axis=0, til...  162 us
    slice x9, local copies, waits for them, and re-layouts, unshare(): pieces.append(whole[offset:offset + amount].reshape(piece_shape))  91.4 us
    all_gather x2, waiting for transfers between devices, layer_forward(): lax.all_gather(keys_local, 'seq', axis=1, tiled=True)  43.6 us
    reshape x1, local copies, waits for them, and re-layouts, share(): flat = flat.reshape(device_count, -1)  38 us
    dot_general x2, matrix products, layer_backward(): jnp.einsum('rqhd,rkhd->rhqk', grad_attended, values_all, preferred_elemen...  37.7 us
  transfers between devices with their start and end apart: 9, of which 3 were waited for; matrix products, arithmetic and copies ran while one was open for 13% of the time, Pallas kernels for 0%

commit v1 on v0

v1 whole, which is shorter than its diff:
```python
import functools
import jax, jax.numpy as jnp
from jax import lax
from jax.experimental import pallas as pl
from jax.experimental.pallas import tpu as pltpu
from jax.sharding import PartitionSpec as P

bf16, f32 = jnp.bfloat16, jnp.float32
QB = 256
LANES = 128
BIG = 1e30
NT = (((1,), (1,)), ((), ()))


def dot(a, b):
    return lax.dot_general(a, b, (((1,), (0,)), ((), ())), preferred_element_type=f32)


def dot_nt(a, b):
    return lax.dot_general(a, b, NT, preferred_element_type=f32)


OTHER_LENGTHS = (0, 128, 256, 512)


def window_plan(own_segments, other_segments, half):
    n = own_segments.shape[0]
    blocks = n // QB
    first, last = own_segments[::QB], own_segments[QB - 1 :: QB]
    rows = []
    for b in range(blocks):
        overlap = (own_segments >= first[b]) & (own_segments <= last[b])
        outside = (jnp.arange(n) // QB) != b
        wide = jnp.any(overlap & outside)
        hit = (other_segments >= first[b]) & (other_segments <= last[b])
        count = jnp.sum(hit.astype(jnp.int32))
        code = sum((count > length).astype(jnp.int32) for length in OTHER_LENGTHS[:-1])
        rows.append(code * 2 + wide.astype(jnp.int32))
    return jnp.concatenate([jnp.stack(rows), jnp.reshape(half, (1,)).astype(jnp.int32)])


def query_features(segments):
    lane = jnp.arange(LANES) % 64
    other = (segments[:, None] != lane[None, :]) & (lane < 4)[None, :]
    return jnp.where(other, BIG, 0.0).astype(bf16)


def key_features(segments):
    lane = jnp.arange(LANES) % 64
    same = (segments[:, None] == lane[None, :]) & (lane < 4)[None, :]
    return jnp.where(same, -1.0, jnp.where((lane >= 4) & (lane < 7), 1.0, 0.0)[None, :]).astype(bf16)


def per_window(plan_ref, b, body):
    code = plan_ref[b]
    upper = plan_ref[2] == 1
    for c, length in enumerate(OTHER_LENGTHS):
        for wide in (0, 1):
            @pl.when(code == c * 2 + wide)
            def _(length=length, wide=wide):
                own_start = 0 if wide else pl.multiple_of(b * QB, QB)
                own_length = 2 * QB if wide else QB
                other_start = pl.multiple_of(jnp.where(upper, 2 * QB - length, 0), 128)
                body(own_start, own_length, other_start, length)


def forward_kernel(plan, q, k, v, ko, vo, qf, kf, kfo, out, lse, k2, v2):
    pair = pl.program_id(0)
    lane = lax.broadcasted_iota(jnp.int32, (1, LANES), 1)
    low = lane < 64
    n = k.shape[0]
    one = jnp.ones((1, LANES), bf16)
    for part, (kr, vr, fr) in enumerate(((k, v, kf), (ko, vo, kfo))):
        rows = pl.ds(part * n, n)
        kk, vv, ff = kr[...], vr[...], fr[...]
        k2[0, rows] = jnp.where(low, kk, ff)
        k2[1, rows] = jnp.where(low, ff, kk)
        v2[0, rows] = jnp.where(low, vv, one)
        v2[1, rows] = jnp.where(low, one, vv)

    @pl.when(pair == 0)
    def _():
        lse[...] = jnp.zeros_like(lse)

    @pl.loop(0, n // QB)
    def _(b):
        qrows = pl.ds(pl.multiple_of(b * QB, QB), QB)

        def body(own_start, own_length, other_start, other_length):
            qq, feature = q[qrows] * jnp.bfloat16(0.125), qf[qrows]
            results = []
            for h in range(2):
                queries = jnp.where(low, qq, feature) if h == 0 else jnp.where(low, feature, qq)
                own = pl.ds(own_start, own_length)
                s = [dot_nt(queries, k2[h, own])]
                if other_length:
                    other = pl.ds(n + other_start, other_length)
                    s.append(dot_nt(queries, k2[h, other]))
                top = functools.reduce(jnp.maximum, [jnp.max(x, axis=1, keepdims=True) for x in s])
                p = [jnp.exp(x - top).astype(bf16) for x in s]
                acc = dot(p[0], v2[h, own])
                if other_length:
                    acc = acc + dot(p[1], v2[h, other])
                results.append((top, acc))
            (top_a, acc_a), (top_b, acc_b) = results
            total = pltpu.roll(jnp.where(low, acc_b, acc_a), 64, 1)
            out[qrows] = (jnp.where(low, acc_a, acc_b) / total).astype(bf16)
            logs = jnp.where(low, top_a, top_b) + jnp.log(total)
            spread = jnp.where(lane == 2 * pair, logs[:, 0:1], jnp.where(lane == 2 * pair + 1, logs[:, 64:65], lse[qrows]))
            lse[qrows] = spread

        per_window(plan, b, body)


def attention_forward(plan, queries, kv, kv_other, qf, kf, kfo):
    n, width = queries.shape
    pairs = width // LANES
    block = lambda off: pl.BlockSpec((n, LANES), lambda p, *_: (0, off + p))
    fixed = pl.BlockSpec((n, LANES), lambda p, *_: (0, 0))
    return pl.pallas_call(
        forward_kernel,
        grid_spec=pltpu.PrefetchScalarGridSpec(
            num_scalar_prefetch=1,
            grid=(pairs,),
            in_specs=[block(0), block(0), block(pairs), block(0), block(pairs), fixed, fixed, fixed],
            out_specs=[block(0), fixed],
            scratch_shapes=[pltpu.VMEM((2, 2 * n, LANES), bf16), pltpu.VMEM((2, 2 * n, LANES), bf16)],
        ),
        out_shape=[jax.ShapeDtypeStruct((n, pairs * LANES), bf16), jax.ShapeDtypeStruct((n, LANES), f32)],
        compiler_params=pltpu.CompilerParams(vmem_limit_bytes=24 << 20),
        cost_estimate=pl.CostEstimate(flops=4 * n * 2 * n * pairs * LANES * 2, bytes_accessed=n * LANES * pairs * 14, transcendentals=n * 2 * n * pairs * 2),
        name="attention_forward",
    )(plan, queries, kv, kv, kv_other, kv_other, qf, kf, kfo)


def split3(x):
    hi = x.astype(bf16).astype(f32)
    mid = (x - hi).astype(bf16).astype(f32)
    return hi, mid, x - hi - mid


def backward_kernel(plan, q, k, v, ko, vo, do, o, lse, qf, kf, kfo, dq, dk, dv, dko, dvo, k2, v2, kt, q2, do2, dks, dvs):
    pair = pl.program_id(0)
    lane = lax.broadcasted_iota(jnp.int32, (1, LANES), 1)
    low = lane < 64
    n = k.shape[0]
    sub = lane % 64
    for part, (kr, vr, fr) in enumerate(((k, v, kf), (ko, vo, kfo))):
        rows = pl.ds(part * n, n)
        kk, vv, ff = kr[...], vr[...], fr[...]
        k2[0, rows] = jnp.where(low, kk, ff)
        k2[1, rows] = jnp.where(low, ff, kk)
        v2[0, rows] = jnp.where(low, vv, ff)
        v2[1, rows] = jnp.where(low, ff, vv)
        kt[:, rows] = kk.astype(f32).T.astype(bf16)
    qq = q[...] * jnp.bfloat16(0.125)
    feature = qf[...]
    dd = do[...]
    product = dd.astype(f32) * o[...].astype(f32)
    logs = lse[...]
    for h in range(2):
        mine = low if h == 0 else jnp.logical_not(low)
        head_lse = jnp.sum(jnp.where(lane == 2 * pair + h, logs, 0.0), axis=1, keepdims=True)
        delta = jnp.sum(jnp.where(mine, product, 0.0), axis=1, keepdims=True)
        a, b, c = split3(-head_lse)
        extra = jnp.where(sub == 4, a, jnp.where(sub == 5, b, jnp.where(sub == 6, c, feature.astype(f32)))).astype(bf16)
        q2[h] = jnp.where(mine, qq, extra)
        a, b, c = split3(-delta)
        extra = jnp.where(sub == 4, a, jnp.where(sub == 5, b, jnp.where(sub == 6, c, 0.0))).astype(bf16)
        do2[h] = jnp.where(mine, dd, extra)
    dks[...] = jnp.zeros_like(dks)
    dvs[...] = jnp.zeros_like(dvs)

    @pl.loop(0, n // QB)
    def _(b):
        qrows = pl.ds(pl.multiple_of(b * QB, QB), QB)

        def body(own_start, own_length, other_start, other_length):
            gradients = []
            d_pair = do[qrows]
            q_pair = q[qrows] * jnp.bfloat16(0.125)
            windows = [pl.ds(own_start, own_length)]
            if other_length:
                windows.append(pl.ds(n + other_start, other_length))
            total = [None, None]
            for win in windows:
                terms_v, terms_k = [], []
                for h in range(2):
                    queries, outward = q2[h, qrows], do2[h, qrows]
                    p = jnp.exp(dot_nt(k2[h, win], queries))
                    ds = (p * dot_nt(v2[h, win], outward)).astype(bf16)
                    terms_v.append(dot(p.astype(bf16), d_pair))
                    terms_k.append(dot(ds, q_pair))
                    part = dot(kt[h * 64 : h * 64 + 64, win], ds)
                    total[h] = part if total[h] is None else total[h] + part
                dvs[win] += jnp.where(low, terms_v[0], terms_v[1])
                dks[win] += jnp.where(low, terms_k[0], terms_k[1])
            both = jnp.concatenate(total, axis=0) * 0.125
            dq[qrows] = both.T.astype(bf16)

        per_window(plan, b, body)

    dk[...] = dks[0:n].astype(bf16)
    dv[...] = dvs[0:n].astype(bf16)
    dko[...] = dks[n : 2 * n].astype(bf16)
    dvo[...] = dvs[n : 2 * n].astype(bf16)


def attention_backward(plan, queries, kv, kv_other, d_out, out, lse, qf, kf, kfo):
    n, width = queries.shape
    pairs = width // LANES
    block = lambda off: pl.BlockSpec((n, LANES), lambda p, *_: (0, off + p))
    fixed = pl.BlockSpec((n, LANES), lambda p, *_: (0, 0))
    shape = jax.ShapeDtypeStruct((n, pairs * LANES), bf16)
    return pl.pallas_call(
        backward_kernel,
        grid_spec=pltpu.PrefetchScalarGridSpec(
            num_scalar_prefetch=1,
            grid=(pairs,),
            in_specs=[block(0), block(0), block(pairs), block(0), block(pairs), block(0), block(0), fixed, fixed, fixed, fixed],
            out_specs=[block(0)] * 5,
            scratch_shapes=[
                pltpu.VMEM((2, 2 * n, LANES), bf16),
                pltpu.VMEM((2, 2 * n, LANES), bf16),
                pltpu.VMEM((LANES, 2 * n), bf16),
                pltpu.VMEM((2, n, LANES), bf16),
                pltpu.VMEM((2, n, LANES), bf16),
                pltpu.VMEM((2 * n, LANES), f32),
                pltpu.VMEM((2 * n, LANES), f32),
            ],
        ),
        out_shape=[shape] * 5,
        compiler_params=pltpu.CompilerParams(vmem_limit_bytes=32 << 20),
        cost_estimate=pl.CostEstimate(flops=10 * n * 2 * n * pairs * LANES * 2, bytes_accessed=n * LANES * pairs * 24, transcendentals=n * 2 * n * pairs * 2),
        name="attention_backward",
    )(plan, queries, kv, kv, kv_other, kv_other, d_out, out, lse, qf, kf, kfo)


LAYERS = 2
EPSILON = 1e-05
GELU_SCALE = 0.7978845608028654
GELU_CUBIC = 0.044715
AXES = ("batch", "seq")
SEQ_BIT, CORE_BIT = 0, 1


def norm_forward(v, gain, shift):
    offset = v - jnp.mean(v, axis=-1, keepdims=True)
    root = lax.rsqrt(jnp.mean(offset * offset, axis=-1, keepdims=True) + EPSILON)
    n = offset * root
    return n * gain + shift, n, root


def norm_backward(g, n, root, gain):
    dn = g * gain
    back = root * (dn - jnp.mean(dn, axis=-1, keepdims=True) - n * jnp.mean(dn * n, axis=-1, keepdims=True))
    return back, jnp.sum(g * n, axis=0), jnp.sum(g, axis=0)


def gelu_parts(v):
    t = jnp.tanh(GELU_SCALE * (v + GELU_CUBIC * v * v * v))
    return t


def gelu(v):
    return 0.5 * v * (1.0 + gelu_parts(v))


def gelu_slope(v):
    t = gelu_parts(v)
    return 0.5 * (1.0 + t) + 0.5 * v * (1.0 - t * t) * GELU_SCALE * (1.0 + 3.0 * GELU_CUBIC * v * v)


def tn(a, b):
    return lax.dot_general(a, b, (((0,), (0,)), ((), ())), preferred_element_type=f32)


def token_sum(v):
    return jnp.sum(v.astype(f32), axis=0)


class Wires:
    def __init__(self):
        self.count = lax.axis_size(AXES)
        self.place = lax.axis_index(AXES)
        self.bits = self.count.bit_length() - 1

    def bit(self, b):
        return (self.place >> b) & 1

    def exchange(self, x, b):
        return lax.ppermute(x, AXES, [(i, i ^ (1 << b)) for i in range(self.count)])

    def swap(self, x):
        pairs = [(i, i ^ 3) for i in range(self.count) if i % 4 in (1, 2)]
        moved = lax.ppermute(x, AXES, pairs)
        stays = self.bit(0) == self.bit(1)
        return jnp.where(stays, x, moved)

    def scatter(self, piece, order):
        for b in order:
            half = piece.shape[0] // 2
            keep = lax.dynamic_slice_in_dim(piece, self.bit(b) * half, half, 0)
            send = lax.dynamic_slice_in_dim(piece, (1 - self.bit(b)) * half, half, 0)
            piece = (keep.astype(f32) + self.exchange(send, b).astype(f32)).astype(bf16)
        return piece

    def gather(self, piece, order):
        for b in reversed(order):
            other = self.exchange(piece, b)
            first = self.bit(b) == 0
            piece = jnp.concatenate([jnp.where(first, piece, other), jnp.where(first, other, piece)], axis=0)
        return piece

    def orders(self):
        rest = list(range(2, self.bits))
        if not rest:
            return [[0], [0]]
        return [[0] + rest, rest[:1] + [0] + rest[1:]]


def weight_terms(wires, left, right):
    half = left.shape[1] // 2
    mine = lax.dynamic_slice_in_dim(left, wires.bit(CORE_BIT) * half, half, 1)
    theirs = lax.dynamic_slice_in_dim(left, (1 - wires.bit(CORE_BIT)) * half, half, 1)
    columns = right.shape[1] // 2
    return [(tn(mine, part), tn(theirs, part)) for part in (right[:, :columns], right[:, columns:])]


def add_terms(first, second):
    if first is None:
        return second
    return [tuple(a + b for a, b in zip(x, y)) for x, y in zip(first, second)]


def reduce_weight(wires, terms):
    out = []
    for (mine, theirs), order in zip(terms, wires.orders()):
        arrived = wires.exchange(theirs.astype(bf16), CORE_BIT)
        piece = (mine + arrived.astype(f32)).astype(bf16)
        piece = wires.scatter(piece, order)
        out.append(wires.gather(piece, [CORE_BIT] + order))
    return jnp.concatenate(out, axis=1).astype(f32)


def layer_forward(x, places, wires, weights):
    w_qkv, b_qv, w_out, b_out, gains, shifts, w_in, b_in, w_down, b_down = weights
    plan, qf, kf, kfo = places
    width = x.shape[-1]
    x_low = x.astype(bf16)
    bias = jnp.concatenate([jnp.zeros_like(b_qv[1]), b_qv[1]])
    kv = (jnp.dot(x_low, w_qkv[:, width:], preferred_element_type=f32) + bias).astype(bf16)
    kv_other = wires.exchange(kv, CORE_BIT)
    q = (jnp.dot(x_low, w_qkv[:, :width], preferred_element_type=f32) + b_qv[0]).astype(bf16)
    attended, lse = attention_forward(plan, q, kv, kv_other, qf, kf, kfo)
    residual = x + jnp.dot(attended, w_out, preferred_element_type=f32) + b_out
    normalized, n1, r1 = norm_forward(residual, gains[0], shifts[0])
    normalized_low = normalized.astype(bf16)
    inner = jnp.dot(normalized_low, w_in, preferred_element_type=f32) + b_in
    activation = gelu(inner).astype(bf16)
    residual_two = normalized + jnp.dot(activation, w_down, preferred_element_type=f32) + b_down
    out, n2, r2 = norm_forward(residual_two, gains[1], shifts[1])
    return out, (x_low, q, kv, kv_other, attended, lse, n1, r1, normalized_low, inner, activation, n2, r2)


def layer_backward(g, kept, places, wires, weights):
    w_qkv, b_qv, w_out, b_out, gains, shifts, w_in, b_in, w_down, b_down = weights
    plan, qf, kf, kfo = places
    x_low, q, kv, kv_other, attended, lse, n1, r1, normalized_low, inner, activation, n2, r2 = kept
    width = g.shape[-1]
    g_two, gain_two, shift_two = norm_backward(g, n2, r2, gains[1])
    branch_two = g_two.astype(bf16)
    d_down = weight_terms(wires, activation, branch_two)
    d_b_down = token_sum(branch_two)
    d_act = lax.dot_general(branch_two, w_down, NT, preferred_element_type=f32)
    d_inner = (gelu_slope(inner) * d_act).astype(bf16)
    d_b_in = token_sum(d_inner)
    d_in = weight_terms(wires, normalized_low, d_inner)
    g_norm = g_two + lax.dot_general(d_inner, w_in, NT, preferred_element_type=f32)
    g_res, gain_one, shift_one = norm_backward(g_norm, n1, r1, gains[0])
    branch = g_res.astype(bf16)
    d_b_out = token_sum(branch)
    d_out = weight_terms(wires, attended, branch)
    d_attended = lax.dot_general(branch, w_out, NT, preferred_element_type=f32).astype(bf16)
    dq, dk, dv, dko, dvo = attention_backward(plan, q, kv, kv_other, d_attended, attended, lse, qf, kf, kfo)
    arrived_k, arrived_v = wires.exchange(dko, CORE_BIT), wires.exchange(dvo, CORE_BIT)
    dk = (dk.astype(f32) + arrived_k.astype(f32)).astype(bf16)
    dv = (dv.astype(f32) + arrived_v.astype(f32)).astype(bf16)
    packed = jnp.concatenate([dq, dk, dv], axis=-1)
    d_qkv = weight_terms(wires, x_low, packed)
    g = g_res + lax.dot_general(packed, w_qkv, NT, preferred_element_type=f32)
    small = jnp.concatenate([token_sum(dq), token_sum(dv), d_b_out, gain_one, gain_two, shift_one, shift_two, d_b_in, d_b_down])
    return g, (d_down, d_in, d_out, d_qkv), small


def per_device(hidden_in, segment_ids, w_qkv, b_qv, w_out, b_out, gains, shifts, w_in, b_in, w_down, b_down, out_grad):
    weights = (w_qkv, b_qv, w_out, b_out, gains, shifts, w_in, b_in, w_down, b_down)
    wires = Wires()
    width = hidden_in.shape[-1]
    start = wires.swap(hidden_in[0])
    segments = wires.swap(segment_ids[0])
    g_last = wires.swap(out_grad[0])
    n = start.shape[0]
    core = wires.bit(CORE_BIT)
    own = lax.dynamic_slice_in_dim(segments, core * n, n, 0)
    other = lax.dynamic_slice_in_dim(segments, (1 - core) * n, n, 0)
    places = (window_plan(own, other, core), query_features(own), key_features(own), key_features(other))
    x = start.astype(f32)
    kept = []
    for _ in range(LAYERS):
        x, saved = layer_forward(x, places, wires, weights)
        kept.append(saved)
    hidden_out = wires.swap(x.astype(bf16))
    g = g_last.astype(f32)
    terms, small = [None] * 4, 0.0
    for saved in reversed(kept):
        g, new_terms, new_small = layer_backward(g, saved, places, wires, weights)
        terms = [add_terms(a, b) for a, b in zip(terms, new_terms)]
        small = small + new_small
    for b in range(wires.bits):
        small = small + wires.exchange(small, b)
    d_down, d_in, d_out, d_qkv = [reduce_weight(wires, t) for t in terms]
    input_grad = wires.swap(g.astype(bf16))
    ff = w_in.shape[1]
    rows = jnp.split(small, [2 * width, 3 * width, 5 * width, 7 * width, 7 * width + ff])
    return (
        hidden_out[None],
        input_grad[None],
        d_qkv,
        rows[0].reshape(2, width),
        d_out,
        rows[1],
        rows[2].reshape(2, width),
        rows[3].reshape(2, width),
        d_in,
        rows[4],
        d_down,
        rows[5],
    )


def solution(mesh):
    tokens, copied = P("batch", "seq", None), P()
    return jax.shard_map(
        per_device,
        mesh=mesh,
        in_specs=(tokens, P("batch", None)) + (copied,) * 10 + (tokens,),
        out_specs=(tokens, tokens) + (copied,) * 10,
        check_vma=False,
    )
```

time: 1810 us -> 590 us (0.33)
  blocking collectives: 457 us -> 0 us
  local copies, waits for them, and re-layouts: 453 us -> 20.3 us
  other arithmetic: 391 us -> 90.6 us
  matrix products: 266 us -> 109 us
  starting transfers between devices: 0.37 us -> 142 us
  Pallas kernels: 0 us -> 69.1 us
  waiting for transfers between devices: 205 us -> 141 us
    unnamed x1 -> x0, blocking collectives: 457 us -> none
    convert_element_type x5 -> x43, other arithmetic: 345 us -> 61.4 us  [the longest x4 57.9 us: reduce_weight(): return jnp.concatenate(out, axis=1).astype(f32)]
    unnamed x226 -> x136, local copies, waits for them, and re-layouts: 252 us -> 13.2 us
    all_gather x5 -> x0, waiting for transfers between devices: 205 us -> none  [the longest x1 162 us: unshare(): lax.all_gather(shares.astype(jnp.bfloat16), ('batch', 'seq'), axis=0, til...]
    dot_general x36 -> x50, matrix products: 266 us -> 109 us  [the longest x32 45.2 us: tn(): lax.dot_general(a, b, (((0,), (0,)), ((), ())), preferred_element_type=f32)]
    ppermute x0 -> x96, starting transfers between devices: none -> 142 us  [the longest x91 137 us: exchange(): return lax.ppermute(x, AXES, [(i, i ^ 1 << b) for i in range(self.count)])]
    ppermute x0 -> x96, waiting for transfers between devices: none -> 141 us  [the longest x91 141 us: exchange(): return lax.ppermute(x, AXES, [(i, i ^ 1 << b) for i in range(self.count)])]
    slice x15 -> x6, local copies, waits for them, and re-layouts: 94.7 us -> 2.97 us  [the longest x2 1.17 us: window_plan(): hit = (other_segments >= first[b]) & (other_segments <= last[b])]
  transfers between devices with their start and end apart: 9 -> 96, of which waited for: 3 -> 43; matrix products, arithmetic and copies ran while one was open for 13% -> 26% of each run, Pallas kernels for 0% -> 9%
where the time goes in v1:
time: 590 us; the launch traced here: 581 us
  starting transfers between devices  142 us (24%)
  waiting for transfers between devices  141 us (24%)
  matrix products  109 us (18%)
  other arithmetic  90.6 us (15%)
  Pallas kernels  69.1 us (12%)
  local copies, waits for them, and re-layouts  20.3 us (3%)
  between operations  8.31 us (1%)
    ppermute x91, waiting for transfers between devices, exchange(): return lax.ppermute(x, AXES, [(i, i ^ 1 << b) for i in range(self.count)])  141 us
    ppermute x91, starting transfers between devices, exchange(): return lax.ppermute(x, AXES, [(i, i ^ 1 << b) for i in range(self.count)])  137 us
    convert_element_type x4, other arithmetic, reduce_weight(): return jnp.concatenate(out, axis=1).astype(f32)  57.9 us
    dot_general x32, matrix products, tn(): lax.dot_general(a, b, (((0,), (0,)), ((), ())), preferred_element_type=f32)  45.2 us
    pallas_call x2, Pallas kernels, attention_backward(): pl.pallas_call(backward_kernel, grid_spec=pltpu.PrefetchScalarGridSpec(nu...  39.2 us
    pallas_call x2, Pallas kernels, attention_forward(): pl.pallas_call(forward_kernel, grid_spec=pltpu.PrefetchScalarGridSpec(num...  29.9 us
    dot_general x2, matrix products, layer_backward(): d_act = lax.dot_general(branch_two, w_down, NT, preferred_element_type=f32)  17.4 us
    dot_general x2, matrix products, layer_forward(): inner = jnp.dot(normalized_low, w_in, preferred_element_type=f32) + b_in  15.5 us
  transfers between devices with their start and end apart: 96, of which 43 were waited for; matrix products, arithmetic and copies ran while one was open for 26% of the time, Pallas kernels for 9%

profile of v1, /device:TPU:0, one launch (start us, length us, event | category | flops | bytes accessed | tf_op | source)
XLA Modules:
  0.0 581.0 jit_solution(3025349738569017935)
XLA Ops:
  6.0 3.1 fusion.16.k.v
  9.0 11.9 %collective-permute-start.2 = (bf16[512,1536]{1,0:T(8,128)(2,1)S(1)}, bf16[512,1536]{1,0:T(8,128)(2,1)}, u32[]{:S(2)}, u32[]{:S(2)}) collective-permute-start(bf16[512,1536]{1,0:T(8,128)(2,1)S(1)} %fusion.16.k.v), channel_id=1, source_target_pairs={{0,2},{1,3},{2,0},{3,1},{4,6},{5,7},{6,4},{7,5},{8,10},{9,11},{10,... | collective-permute-start | bytes 4718600 | tf_op jit(solution)/shard_map/ppermute | solution.py:292
  22.4 3.3 convert_reduce_fusion.12
  29.6 3.3 fusion.183
  34.6 2.3 add_convert_fusion.11.q
  38.7 15.1 %attention_forward.2 = (bf16[512,768]{1,0:T(8,128)(2,1)S(1)}, f32[512,128]{1,0:T(8,128)S(1)}) custom-call(s32[3]{0:T(128)S(1)} %pad_add_fusion.plan, bf16[512,768]{1,0:T(8,128)(2,1)S(1)} %add_convert_fusion.11.q, bf16[512,1536]{1,0:T(8,128)(2,1)S(1)} %copy-done.3, bf16[512,1536]{1,0:T(8,128)(2,1)S(1)} %copy-done.3, ...), custom_call_target="tpu_custom_call" | custom-call | flops 3221225472 | bytes 5505024 | tf_op jit(solution)/shard_map/attention_forward/pallas_call | solution.py:120
  55.7 9.3 %multiply_convert_fusion.1 = (bf16[512,3072]{1,0:T(8,128)(2,1)S(1)}, f32[512,3072]{1,0:T(8,128)}) fusion(f32[3072]{0:T(1024)S(1)} %copy-done.47, bf16[512,768]{1,0:T(8,128)(2,1)S(1)} %fusion.52, bf16[768,3072]{1,0:T(8,128)(2,1)} %param.21), kind=kOutput, calls=%fused_computation.21 | convolution fusion | flops 2431647744 | bytes 14954496 | tf_op jit(solution)/shard_map/dot_general | solution.py:359
  65.1 2.7 fusion.201
  70.4 2.5 fusion.17.k.v
  76.8 14.9 %attention_forward.3 = (bf16[512,768]{1,0:T(8,128)(2,1)S(1)}, f32[512,128]{1,0:T(8,128)S(1)}) custom-call(s32[3]{0:T(128)S(1)} %pad_add_fusion.plan, bf16[512,768]{1,0:T(8,128)(2,1)S(1)} %add_convert_fusion.10.q, bf16[512,1536]{1,0:T(8,128)(2,1)} %fusion.17.k.v, bf16[512,1536]{1,0:T(8,128)(2,1)} %fusion.17.k.v, ...), custom_call_target="tpu_custom_call" | custom-call | flops 3221225472 | bytes 5505024 | tf_op jit(solution)/shard_map/attention_forward/pallas_call | solution.py:120
  93.4 6.2 %multiply_convert_fusion = (bf16[512,3072]{1,0:T(8,128)(2,1)S(1)}, f32[512,3072]{1,0:T(8,128)}) fusion(f32[3072]{0:T(1024)S(1)} %copy-done.47, bf16[512,768]{1,0:T(8,128)(2,1)S(1)} %fusion.54, bf16[768,3072]{1,0:T(8,128)(2,1)S(1)} %bitcast.55), kind=kOutput, calls=%fused_computation.20 | convolution fusion | flops 2431647744 | bytes 14954496 | tf_op jit(solution)/shard_map/dot_general | solution.py:359
  99.7 2.8 fusion.203
  105.6 8.0 %convert_reduce_fusion.1 = (f32[3072]{0:T(1024)S(1)}, bf16[512,3072]{1,0:T(8,128)(2,1)S(1)}) fusion(bf16[512,768]{1,0:T(8,128)(2,1)S(1)} %get-tuple-element.75, bf16[3072,768]{1,0:T(8,128)(2,1)S(1)} %bitcast.53, f32[512,3072]{1,0:T(8,128)} %get-tuple-element.184, f32[3072]{0:T(1024)S(1)} %copy-done.47), kind=kOutput, calls=%fused_computation.19 | convolution fusion | flops 2450519040 | bytes 14966784 | tf_op jit(solution)/shard_map/dot_general | solution.py:375
  113.6 3.4 multiply_reduce_fusion.2
  119.7 2.4 fusion.73
  122.2 2.5 fusion.75
  127.5 19.7 %attention_backward.2 = (bf16[512,768]{1,0:T(8,128)(2,1)S(1)}, bf16[512,768]{1,0:T(8,128)(2,1)S(1)}, bf16[512,768]{1,0:T(8,128)(2,1)S(1)}, bf16[512,768]{1,0:T(8,128)(2,1)S(1)}, bf16[512,768]{1,0:T(8,128)(2,1)S(1)}) custom-call(s32[3]{0:T(128)S(1)} %pad_add_fusion.plan, bf16[512,768]{1,0:T(8,128)(2,1)S(1)} %add_convert_fusion.10.q, ...), custom_call_target="tpu_custom_call" | custom-call | flops 8053063680 | bytes 9437184 | tf_op jit(solution)/shard_map/attention_backward/pallas_call | solution.py:215
  147.2 3.3 collective-permute-start.7
  152.8 2.5 fusion.83
  155.4 2.5 fusion.85
  165.5 2.5 multiply_reduce_fusion
  168.7 9.4 %convert_reduce_fusion = (f32[3072]{0:T(1024)S(1)}, bf16[512,3072]{1,0:T(8,128)(2,1)S(1)}) fusion(bf16[512,768]{1,0:T(8,128)(2,1)S(1)} %get-tuple-element.67, bf16[3072,768]{1,0:T(8,128)(2,1)} %param.23, f32[512,3072]{1,0:T(8,128)} %get-tuple-element.178, f32[3072]{0:T(1024)S(1)} %copy-done.47), kind=kOutput, calls=%fused_computation.18 | convolution fusion | flops 2450519040 | bytes 14966784 | tf_op jit(solution)/shard_map/dot_general | solution.py:375
  178.2 3.2 multiply_reduce_fusion.1
  186.4 19.5 %attention_backward.3 = (bf16[512,768]{1,0:T(8,128)(2,1)S(1)}, bf16[512,768]{1,0:T(8,128)(2,1)S(1)}, bf16[512,768]{1,0:T(8,128)(2,1)S(1)}, bf16[512,768]{1,0:T(8,128)(2,1)S(1)}, bf16[512,768]{1,0:T(8,128)(2,1)S(1)}) custom-call(s32[3]{0:T(128)S(1)} %pad_add_fusion.plan, bf16[512,768]{1,0:T(8,128)(2,1)S(1)} %copy-done.6, bf16[512,1536]{1,0:T(8,128)(2,1)S(1)} %copy-done.4, ...), custom_call_target="tpu_custom_call" | custom-call | flops 8053063680 | bytes 9437184 | tf_op jit(solution)/shard_map/attention_backward/pallas_call | solution.py:215
  221.6 6.6 %collective-permute-start.47 = (bf16[192,384]{1,0:T(8,128)(2,1)S(1)}, bf16[192,384]{1,0:T(8,128)(2,1)S(1)}, u32[]{:S(2)}, u32[]{:S(2)}) collective-permute-start(bf16[192,384]{1,0:T(8,128)(2,1)S(1)} %constant_dynamic-slice_fusion.20), channel_id=1, source_target_pairs={{0,4},{1,5},{2,6},{3,7},{4,0},{5,1},{6,2},{7,3},{8,12},{9,13},{10,... | collective-permute-start | bytes 442376 | tf_op jit(solution)/shard_map/ppermute | solution.py:292
  228.6 3.6 collective-permute-done.47
  232.2 12.9 %collective-permute-start.37 = (bf16[192,384]{1,0:T(8,128)(2,1)S(1)}, bf16[192,384]{1,0:T(8,128)(2,1)S(1)}, u32[]{:S(2)}, u32[]{:S(2)}) collective-permute-start(bf16[192,384]{1,0:T(8,128)(2,1)S(1)} %constant_dynamic-slice_fusion.25), channel_id=1, source_target_pairs={{0,1},{1,0},{2,3},{3,2},{4,5},{5,4},{6,7},{7,6},{8,9},{9,8},{10,11... | collective-permute-start | bytes 442376 | tf_op jit(solution)/shard_map/ppermute | solution.py:292
  245.2 3.9 collective-permute-done.37
  250.9 2.5 collective-permute-done.48
  255.0 2.8 collective-permute-done.38
  257.8 2.3 collective-permute-start.49
  267.3 3.4 collective-permute-done.50
  271.9 3.4 collective-permute-done.40
  276.6 3.4 collective-permute-done.51
  281.3 3.4 collective-permute-done.41
  294.7 2.5 collective-permute-done.53
  298.7 2.8 collective-permute-done.43
  305.9 2.9 add_convert_fusion.4
  320.9 2.5 collective-permute-done.33
  329.8 2.7 collective-permute-done.35
  342.5 2.4 add_convert_fusion.2
  346.0 2.4 add_convert_fusion
  361.0 3.6 collective-permute-done.67
  370.0 7.4 %collective-permute-done.87 = bf16[768,384]{1,0:T(8,128)(2,1)S(1)} collective-permute-done((bf16[768,384]{1,0:T(8,128)(2,1)S(1)}, bf16[768,384]{1,0:T(8,128)(2,1)S(1)}, u32[]{:S(2)}, u32[]{:S(2)}) %collective-permute-start.87) | collective-permute-done | bytes 589856 | tf_op jit(solution)/shard_map/ppermute | solution.py:292
  378.1 2.3 collective-permute-done.77
  382.6 13.6 %collective-permute-done.68 = bf16[96,1536]{1,0:T(8,128)(2,1)S(1)} collective-permute-done((bf16[96,1536]{1,0:T(8,128)(2,1)S(1)}, bf16[96,1536]{1,0:T(8,128)(2,1)S(1)}, u32[]{:S(2)}, u32[]{:S(2)}) %collective-permute-start.68) | collective-permute-done | bytes 294944 | tf_op jit(solution)/shard_map/ppermute | solution.py:292
  399.6 2.3 collective-permute-done.88
  409.9 2.7 collective-permute-done.89
  413.1 2.9 collective-permute-done.79
  416.7 2.7 collective-permute-start.80
  420.3 4.4 collective-permute-done.90
  429.5 3.5 collective-permute-start.24
  443.3 6.0 %collective-permute-done.25 = bf16[24,1152]{1,0:T(8,128)(2,1)S(1)} collective-permute-done((bf16[24,1152]{1,0:T(8,128)(2,1)S(1)}, bf16[24,1152]{1,0:T(8,128)(2,1)S(1)}, u32[]{:S(2)}, u32[]{:S(2)}) %collective-permute-start.25) | collective-permute-done | bytes 55328 | tf_op jit(solution)/shard_map/ppermute | solution.py:292
  449.3 3.4 collective-permute-start.15
  452.7 3.2 collective-permute-done.15
  455.9 2.5 collective-permute-start.26
  463.7 4.0 collective-permute-start.27
  467.8 2.7 collective-permute-done.27
  472.5 2.7 collective-permute-done.17
  485.4 24.8 %collective-permute-done.29 = bf16[192,1152]{1,0:T(8,128)(2,1)S(1)} collective-permute-done((bf16[192,1152]{1,0:T(8,128)(2,1)S(1)}, bf16[192,1152]{1,0:T(8,128)(2,1)S(1)}, u32[]{:S(2)}, u32[]{:S(2)}) %collective-permute-start.29) | collective-permute-done | bytes 442400 | tf_op jit(solution)/shard_map/ppermute | solution.py:292
  512.2 6.3 %collective-permute-done.19 = bf16[192,1152]{1,0:T(8,128)(2,1)S(1)} collective-permute-done((bf16[192,1152]{1,0:T(8,128)(2,1)S(1)}, bf16[192,1152]{1,0:T(8,128)(2,1)S(1)}, u32[]{:S(2)}, u32[]{:S(2)}) %collective-permute-start.19) | collective-permute-done | bytes 442400 | tf_op jit(solution)/shard_map/ppermute | solution.py:292
  522.6 15.7 %maximum_convert_fusion.2 = f32[768,2304]{1,0:T(8,128)} fusion(bf16[384,1152]{1,0:T(8,128)(2,1)S(1)} %get-tuple-element.96, bf16[384,1152]{1,0:T(8,128)(2,1)S(1)} %get-tuple-element.95, bf16[384,1152]{1,0:T(8,128)(2,1)S(1)} %get-tuple-element.94, bf16[384,1152]{1,0:T(8,128)(2,1)S(1)} %get-tuple-element.93), kind=kLoop, calls=%fused_computation.24 | loop fusion | flops 14155776 | bytes 10616832 | tf_op jit(solution)/shard_map/convert_element_type | solution.py:343
  539.6 21.4 %maximum_convert_fusion = f32[768,3072]{1,0:T(8,128)} fusion(bf16[384,1536]{1,0:T(8,128)(2,1)S(1)} %get-tuple-element.92, bf16[384,1536]{1,0:T(8,128)(2,1)S(1)} %get-tuple-element.91, bf16[384,1536]{1,0:T(8,128)(2,1)S(1)} %get-tuple-element.90, bf16[384,1536]{1,0:T(8,128)(2,1)S(1)} %get-tuple-element.89), kind=kLoop, calls=%fused_computation.22 | loop fusion | flops 18874368 | bytes 14155776 | tf_op jit(solution)/shard_map/convert_element_type | solution.py:343
  561.5 19.2 %maximum_convert_fusion.1 = f32[3072,768]{1,0:T(8,128)} fusion(bf16[1536,384]{1,0:T(8,128)(2,1)S(1)} %get-tuple-element.88, bf16[1536,384]{1,0:T(8,128)(2,1)S(1)} %get-tuple-element.87, bf16[1536,384]{1,0:T(8,128)(2,1)S(1)} %get-tuple-element.86, bf16[1536,384]{1,0:T(8,128)(2,1)S(1)} %get-tuple-element.85), kind=kLoop, calls=%fused_computation.23 | loop fusion | flops 18874368 | bytes 14155776 | tf_op jit(solution)/shard_map/convert_element_type | solution.py:343
  (532 shorter events, 192.4 us)
Async XLA Ops:
  1.5 19.4 %collective-permute-start.1 = (s32[1024]{0:T(1024)}, s32[1024]{0:T(1024)S(1)}, u32[]{:S(2)}, u32[]{:S(2)}) collective-permute-start(s32[1024]{0:T(1024)} %bitcast.48), channel_id=1, source_target_pairs={{1,2},{2,1},{5,6},{6,5},{9,10},{10,9},{13,14},{14,13},{17,18},{18,... | collective-permute-start | bytes 12296 | tf_op jit(solution)/shard_map/ppermute | solution.py:296
  9.0 27.9 %collective-permute-start.2 = (bf16[512,1536]{1,0:T(8,128)(2,1)S(1)}, bf16[512,1536]{1,0:T(8,128)(2,1)}, u32[]{:S(2)}, u32[]{:S(2)}) collective-permute-start(bf16[512,1536]{1,0:T(8,128)(2,1)S(1)} %fusion.16.k.v), channel_id=1, source_target_pairs={{0,2},{1,3},{2,0},{3,1},{4,6},{5,7},{6,4},{7,5},{8,10},{9,11},{10,... | collective-permute-start | bytes 4718600 | tf_op jit(solution)/shard_map/ppermute | solution.py:292
  73.0 29.8 %collective-permute-start.5 = (bf16[512,768]{1,0:T(8,128)(2,1)}, bf16[512,768]{1,0:T(8,128)(2,1)}, u32[]{:S(2)}, u32[]{:S(2)}) collective-permute-start(bf16[512,768]{1,0:T(8,128)(2,1)} %bitcast.10), channel_id=1, source_target_pairs={{1,2},{2,1},{5,6},{6,5},{9,10},{10,9},{13,14},{14,13},{17,18},{18,... | collective-permute-start | bytes 2359304 | tf_op jit(solution)/shard_map/ppermute | solution.py:296
  124.6 93.9 %collective-permute-start.4 = (bf16[512,768]{1,0:T(8,128)(2,1)S(1)}, bf16[512,768]{1,0:T(8,128)(2,1)}, u32[]{:S(2)}, u32[]{:S(2)}) collective-permute-start(bf16[512,768]{1,0:T(8,128)(2,1)S(1)} %get-tuple-element.97), channel_id=1, source_target_pairs={{1,2},{2,1},{5,6},{6,5},{9,10},{10,9},{13,14},{14,13},{17,18},{18,... | collective-permute-start | bytes 2359304 | tf_op jit(solution)/shard_map/ppermute | solution.py:296
  147.2 13.0 %collective-permute-start.7 = (bf16[512,768]{1,0:T(8,128)(2,1)S(1)}, bf16[512,768]{1,0:T(8,128)(2,1)S(1)}, u32[]{:S(2)}, u32[]{:S(2)}) collective-permute-start(bf16[512,768]{1,0:T(8,128)(2,1)S(1)} %get-tuple-element.33), channel_id=1, source_target_pairs={{0,2},{1,3},{2,0},{3,1},{4,6},{5,7},{6,4},{7,5},{8,10},{9,11},{10,... | collective-permute-start | bytes 2359304 | tf_op jit(solution)/shard_map/ppermute | solution.py:292
  150.6 9.9 %collective-permute-start.6 = (bf16[512,768]{1,0:T(8,128)(2,1)S(1)}, bf16[512,768]{1,0:T(8,128)(2,1)S(1)}, u32[]{:S(2)}, u32[]{:S(2)}) collective-permute-start(bf16[512,768]{1,0:T(8,128)(2,1)S(1)} %get-tuple-element.31), channel_id=1, source_target_pairs={{0,2},{1,3},{2,0},{3,1},{4,6},{5,7},{6,4},{7,5},{8,10},{9,11},{10,... | collective-permute-start | bytes 2359304 | tf_op jit(solution)/shard_map/ppermute | solution.py:292
  205.9 98.1 %collective-permute-start.9 = (bf16[512,768]{1,0:T(8,128)(2,1)S(1)}, bf16[512,768]{1,0:T(8,128)(2,1)S(1)}, u32[]{:S(2)}, u32[]{:S(2)}) collective-permute-start(bf16[512,768]{1,0:T(8,128)(2,1)S(1)} %get-tuple-element.39), channel_id=1, source_target_pairs={{0,2},{1,3},{2,0},{3,1},{4,6},{5,7},{6,4},{7,5},{8,10},{9,11},{10,... | collective-permute-start | bytes 2359304 | tf_op jit(solution)/shard_map/ppermute | solution.py:292
  206.5 95.1 %collective-permute-start.8 = (bf16[512,768]{1,0:T(8,128)(2,1)S(1)}, bf16[512,768]{1,0:T(8,128)(2,1)S(1)}, u32[]{:S(2)}, u32[]{:S(2)}) collective-permute-start(bf16[512,768]{1,0:T(8,128)(2,1)S(1)} %get-tuple-element.37), channel_id=1, source_target_pairs={{0,2},{1,3},{2,0},{3,1},{4,6},{5,7},{6,4},{7,5},{8,10},{9,11},{10,... | collective-permute-start | bytes 2359304 | tf_op jit(solution)/shard_map/ppermute | solution.py:292
  207.1 12.5 %collective-permute-start.46 = (bf16[384,384]{1,0:T(8,128)(2,1)S(1)}, bf16[384,384]{1,0:T(8,128)(2,1)S(1)}, u32[]{:S(2)}, u32[]{:S(2)}) collective-permute-start(bf16[384,384]{1,0:T(8,128)(2,1)S(1)} %fusion.92), channel_id=1, source_target_pairs={{0,2},{1,3},{2,0},{3,1},{4,6},{5,7},{6,4},{7,5},{8,10},{9,11},{10,... | collective-permute-start | bytes 884744 | tf_op jit(solution)/shard_map/ppermute | solution.py:292
  208.1 13.6 %collective-permute-start.36 = (bf16[384,384]{1,0:T(8,128)(2,1)S(1)}, bf16[384,384]{1,0:T(8,128)(2,1)S(1)}, u32[]{:S(2)}, u32[]{:S(2)}) collective-permute-start(bf16[384,384]{1,0:T(8,128)(2,1)S(1)} %fusion.91), channel_id=1, source_target_pairs={{0,2},{1,3},{2,0},{3,1},{4,6},{5,7},{6,4},{7,5},{8,10},{9,11},{10,... | collective-permute-start | bytes 884744 | tf_op jit(solution)/shard_map/ppermute | solution.py:292
  218.6 122.4 %collective-permute-start.66 = (bf16[384,1536]{1,0:T(8,128)(2,1)}, bf16[384,1536]{1,0:T(8,128)(2,1)}, u32[]{:S(2)}, u32[]{:S(2)}) collective-permute-start(bf16[384,1536]{1,0:T(8,128)(2,1)} %fusion.19), channel_id=1, source_target_pairs={{0,2},{1,3},{2,0},{3,1},{4,6},{5,7},{6,4},{7,5},{8,10},{9,11},{10,... | collective-permute-start | bytes 3538952 | tf_op jit(solution)/shard_map/ppermute | solution.py:292
  219.6 128.8 %collective-permute-start.56 = (bf16[384,1536]{1,0:T(8,128)(2,1)}, bf16[384,1536]{1,0:T(8,128)(2,1)}, u32[]{:S(2)}, u32[]{:S(2)}) collective-permute-start(bf16[384,1536]{1,0:T(8,128)(2,1)} %fusion.18), channel_id=1, source_target_pairs={{0,2},{1,3},{2,0},{3,1},{4,6},{5,7},{6,4},{7,5},{8,10},{9,11},{10,... | collective-permute-start | bytes 3538952 | tf_op jit(solution)/shard_map/ppermute | solution.py:292
  221.6 10.6 %collective-permute-start.47 = (bf16[192,384]{1,0:T(8,128)(2,1)S(1)}, bf16[192,384]{1,0:T(8,128)(2,1)S(1)}, u32[]{:S(2)}, u32[]{:S(2)}) collective-permute-start(bf16[192,384]{1,0:T(8,128)(2,1)S(1)} %constant_dynamic-slice_fusion.20), channel_id=1, source_target_pairs={{0,4},{1,5},{2,6},{3,7},{4,0},{5,1},{6,2},{7,3},{8,12},{9,13},{10,... | collective-permute-start | bytes 442376 | tf_op jit(solution)/shard_map/ppermute | solution.py:292
  232.2 16.9 %collective-permute-start.37 = (bf16[192,384]{1,0:T(8,128)(2,1)S(1)}, bf16[192,384]{1,0:T(8,128)(2,1)S(1)}, u32[]{:S(2)}, u32[]{:S(2)}) collective-permute-start(bf16[192,384]{1,0:T(8,128)(2,1)S(1)} %constant_dynamic-slice_fusion.25), channel_id=1, source_target_pairs={{0,1},{1,0},{2,3},{3,2},{4,5},{5,4},{6,7},{7,6},{8,9},{9,8},{10,11... | collective-permute-start | bytes 442376 | tf_op jit(solution)/shard_map/ppermute | solution.py:292
  301.5 43.5 %collective-permute-start.86 = (bf16[1536,384]{1,0:T(8,128)(2,1)}, bf16[1536,384]{1,0:T(8,128)(2,1)}, u32[]{:S(2)}, u32[]{:S(2)}) collective-permute-start(bf16[1536,384]{1,0:T(8,128)(2,1)} %fusion.21), channel_id=1, source_target_pairs={{0,2},{1,3},{2,0},{3,1},{4,6},{5,7},{6,4},{7,5},{8,10},{9,11},{10,... | collective-permute-start | bytes 3538952 | tf_op jit(solution)/shard_map/ppermute | solution.py:292
  301.6 16.6 %collective-permute-start.54 = (bf16[192,384]{1,0:T(8,128)(2,1)S(1)}, bf16[192,384]{1,0:T(8,128)(2,1)S(1)}, u32[]{:S(2)}, u32[]{:S(2)}) collective-permute-start(bf16[192,384]{1,0:T(8,128)(2,1)S(1)} %pad_maximum_fusion.33), channel_id=1, source_target_pairs={{0,4},{1,5},{2,6},{3,7},{4,0},{5,1},{6,2},{7,3},{8,12},{9,13},{10,... | collective-permute-start | bytes 442376 | tf_op jit(solution)/shard_map/ppermute | solution.py:292
  323.4 12.3 %collective-permute-start.55 = (bf16[384,384]{1,0:T(8,128)(2,1)}, bf16[384,384]{1,0:T(8,128)(2,1)}, u32[]{:S(2)}, u32[]{:S(2)}) collective-permute-start(bf16[384,384]{1,0:T(8,128)(2,1)} %pad_maximum_fusion.25), channel_id=1, source_target_pairs={{0,2},{1,3},{2,0},{3,1},{4,6},{5,7},{6,4},{7,5},{8,10},{9,11},{10,... | collective-permute-start | bytes 884744 | tf_op jit(solution)/shard_map/ppermute | solution.py:292
  335.8 15.6 %collective-permute-start.76 = (bf16[1536,384]{1,0:T(8,128)(2,1)}, bf16[1536,384]{1,0:T(8,128)(2,1)S(1)}, u32[]{:S(2)}, u32[]{:S(2)}) collective-permute-start(bf16[1536,384]{1,0:T(8,128)(2,1)} %fusion.20), channel_id=1, source_target_pairs={{0,2},{1,3},{2,0},{3,1},{4,6},{5,7},{6,4},{7,5},{8,10},{9,11},{10,... | collective-permute-start | bytes 3538952 | tf_op jit(solution)/shard_map/ppermute | solution.py:292
  337.5 17.3 %collective-permute-start.10 = (bf16[512,768]{1,0:T(8,128)(2,1)}, bf16[512,768]{1,0:T(8,128)(2,1)S(1)}, u32[]{:S(2)}, u32[]{:S(2)}) collective-permute-start(bf16[512,768]{1,0:T(8,128)(2,1)} %add_convert_fusion.4), channel_id=1, source_target_pairs={{1,2},{2,1},{5,6},{6,5},{9,10},{10,9},{13,14},{14,13},{17,18},{18,... | collective-permute-start | bytes 2359304 | tf_op jit(solution)/shard_map/ppermute | solution.py:296
  341.0 16.2 %collective-permute-start.21 = (bf16[384,1152]{1,0:T(8,128)(2,1)}, bf16[384,1152]{1,0:T(8,128)(2,1)S(1)}, u32[]{:S(2)}, u32[]{:S(2)}) collective-permute-start(bf16[384,1152]{1,0:T(8,128)(2,1)} %fusion.25), channel_id=1, source_target_pairs={{0,2},{1,3},{2,0},{3,1},{4,6},{5,7},{6,4},{7,5},{8,10},{9,11},{10,... | collective-permute-start | bytes 2654216 | tf_op jit(solution)/shard_map/ppermute | solution.py:292
  345.1 14.4 %collective-permute-start.11 = (bf16[384,1152]{1,0:T(8,128)(2,1)S(1)}, bf16[384,1152]{1,0:T(8,128)(2,1)S(1)}, u32[]{:S(2)}, u32[]{:S(2)}) collective-permute-start(bf16[384,1152]{1,0:T(8,128)(2,1)S(1)} %copy-done.38), channel_id=1, source_target_pairs={{0,2},{1,3},{2,0},{3,1},{4,6},{5,7},{6,4},{7,5},{8,10},{9,11},{10,... | collective-permute-start | bytes 2654216 | tf_op jit(solution)/shard_map/ppermute | solution.py:292
  348.4 16.3 %collective-permute-start.67 = (bf16[192,1536]{1,0:T(8,128)(2,1)S(1)}, bf16[192,1536]{1,0:T(8,128)(2,1)S(1)}, u32[]{:S(2)}, u32[]{:S(2)}) collective-permute-start(bf16[192,1536]{1,0:T(8,128)(2,1)S(1)} %constant_dynamic-slice_fusion.11), channel_id=1, source_target_pairs={{0,4},{1,5},{2,6},{3,7},{4,0},{5,1},{6,2},{7,3},{8,12},{9,13},{10,... | collective-permute-start | bytes 1769480 | tf_op jit(solution)/shard_map/ppermute | solution.py:292
  351.4 16.4 %collective-permute-start.57 = (bf16[192,1536]{1,0:T(8,128)(2,1)S(1)}, bf16[192,1536]{1,0:T(8,128)(2,1)S(1)}, u32[]{:S(2)}, u32[]{:S(2)}) collective-permute-start(bf16[192,1536]{1,0:T(8,128)(2,1)S(1)} %constant_dynamic-slice_fusion.15), channel_id=1, source_target_pairs={{0,1},{1,0},{2,3},{3,2},{4,5},{5,4},{6,7},{7,6},{8,9},{9,8},{10,11... | collective-permute-start | bytes 1769480 | tf_op jit(solution)/shard_map/ppermute | solution.py:292
  354.8 22.6 %collective-permute-start.87 = (bf16[768,384]{1,0:T(8,128)(2,1)S(1)}, bf16[768,384]{1,0:T(8,128)(2,1)S(1)}, u32[]{:S(2)}, u32[]{:S(2)}) collective-permute-start(bf16[768,384]{1,0:T(8,128)(2,1)S(1)} %constant_dynamic-slice_fusion.3), channel_id=1, source_target_pairs={{0,4},{1,5},{2,6},{3,7},{4,0},{5,1},{6,2},{7,3},{8,12},{9,13},{10,... | collective-permute-start | bytes 1769480 | tf_op jit(solution)/shard_map/ppermute | solution.py:292
  357.2 23.2 %collective-permute-start.77 = (bf16[768,384]{1,0:T(8,128)(2,1)S(1)}, bf16[768,384]{1,0:T(8,128)(2,1)S(1)}, u32[]{:S(2)}, u32[]{:S(2)}) collective-permute-start(bf16[768,384]{1,0:T(8,128)(2,1)S(1)} %constant_dynamic-slice_fusion.7), channel_id=1, source_target_pairs={{0,1},{1,0},{2,3},{3,2},{4,5},{5,4},{6,7},{7,6},{8,9},{9,8},{10,11... | collective-permute-start | bytes 1769480 | tf_op jit(solution)/shard_map/ppermute | solution.py:292
  359.5 46.5 %collective-permute-start.22 = (bf16[192,1152]{1,0:T(8,128)(2,1)S(1)}, bf16[192,1152]{1,0:T(8,128)(2,1)S(1)}, u32[]{:S(2)}, u32[]{:S(2)}) collective-permute-start(bf16[192,1152]{1,0:T(8,128)(2,1)S(1)} %constant_dynamic-slice_fusion.29), channel_id=1, source_target_pairs={{0,4},{1,5},{2,6},{3,7},{4,0},{5,1},{6,2},{7,3},{8,12},{9,13},{10,... | collective-permute-start | bytes 1327112 | tf_op jit(solution)/shard_map/ppermute | solution.py:292
  364.7 41.8 %collective-permute-start.12 = (bf16[192,1152]{1,0:T(8,128)(2,1)S(1)}, bf16[192,1152]{1,0:T(8,128)(2,1)S(1)}, u32[]{:S(2)}, u32[]{:S(2)}) collective-permute-start(bf16[192,1152]{1,0:T(8,128)(2,1)S(1)} %constant_dynamic-slice_fusion.33), channel_id=1, source_target_pairs={{0,1},{1,0},{2,3},{3,2},{4,5},{5,4},{6,7},{7,6},{8,9},{9,8},{10,11... | collective-permute-start | bytes 1327112 | tf_op jit(solution)/shard_map/ppermute | solution.py:292
  367.8 28.4 %collective-permute-start.68 = (bf16[96,1536]{1,0:T(8,128)(2,1)S(1)}, bf16[96,1536]{1,0:T(8,128)(2,1)S(1)}, u32[]{:S(2)}, u32[]{:S(2)}) collective-permute-start(bf16[96,1536]{1,0:T(8,128)(2,1)S(1)} %constant_dynamic-slice_fusion.10), channel_id=1, source_target_pairs={{0,1},{1,0},{2,3},{3,2},{4,5},{5,4},{6,7},{7,6},{8,9},{9,8},{10,11... | collective-permute-start | bytes 884744 | tf_op jit(solution)/shard_map/ppermute | solution.py:292
  377.3 20.3 %collective-permute-start.58 = (bf16[96,1536]{1,0:T(8,128)(2,1)S(1)}, bf16[96,1536]{1,0:T(8,128)(2,1)S(1)}, u32[]{:S(2)}, u32[]{:S(2)}) collective-permute-start(bf16[96,1536]{1,0:T(8,128)(2,1)S(1)} %constant_dynamic-slice_fusion.14), channel_id=1, source_target_pairs={{0,4},{1,5},{2,6},{3,7},{4,0},{5,1},{6,2},{7,3},{8,12},{9,13},{10,... | collective-permute-start | bytes 884744 | tf_op jit(solution)/shard_map/ppermute | solution.py:292
  380.4 21.6 %collective-permute-start.88 = (bf16[384,384]{1,0:T(8,128)(2,1)S(1)}, bf16[384,384]{1,0:T(8,128)(2,1)S(1)}, u32[]{:S(2)}, u32[]{:S(2)}) collective-permute-start(bf16[384,384]{1,0:T(8,128)(2,1)S(1)} %constant_dynamic-slice_fusion.2), channel_id=1, source_target_pairs={{0,1},{1,0},{2,3},{3,2},{4,5},{5,4},{6,7},{7,6},{8,9},{9,8},{10,11... | collective-permute-start | bytes 884744 | tf_op jit(solution)/shard_map/ppermute | solution.py:292
  397.7 10.0 %collective-permute-start.69 = (bf16[48,1536]{1,0:T(8,128)(2,1)S(1)}, bf16[48,1536]{1,0:T(8,128)(2,1)S(1)}, u32[]{:S(2)}, u32[]{:S(2)}) collective-permute-start(bf16[48,1536]{1,0:T(8,128)(2,1)S(1)} %constant_dynamic-slice_fusion.9), channel_id=1, source_target_pairs={{0,8},{1,9},{2,10},{3,11},{4,12},{5,13},{6,14},{7,15},{8,0},{9,1},... | collective-permute-start | bytes 442376 | tf_op jit(solution)/shard_map/ppermute | solution.py:292
  404.1 8.5 %collective-permute-start.89 = (bf16[192,384]{1,0:T(8,128)(2,1)S(1)}, bf16[192,384]{1,0:T(8,128)(2,1)S(1)}, u32[]{:S(2)}, u32[]{:S(2)}) collective-permute-start(bf16[192,384]{1,0:T(8,128)(2,1)S(1)} %constant_dynamic-slice_fusion.1), channel_id=1, source_target_pairs={{0,8},{1,9},{2,10},{3,11},{4,12},{5,13},{6,14},{7,15},{8,0},{9,1},... | collective-permute-start | bytes 442376 | tf_op jit(solution)/shard_map/ppermute | solution.py:292
  406.0 10.0 %collective-permute-start.79 = (bf16[192,384]{1,0:T(8,128)(2,1)S(1)}, bf16[192,384]{1,0:T(8,128)(2,1)S(1)}, u32[]{:S(2)}, u32[]{:S(2)}) collective-permute-start(bf16[192,384]{1,0:T(8,128)(2,1)S(1)} %constant_dynamic-slice_fusion.5), channel_id=1, source_target_pairs={{0,8},{1,9},{2,10},{3,11},{4,12},{5,13},{6,14},{7,15},{8,0},{9,1},... | collective-permute-start | bytes 442376 | tf_op jit(solution)/shard_map/ppermute | solution.py:292
  406.5 21.3 %collective-permute-start.23 = (bf16[96,1152]{1,0:T(8,128)(2,1)S(1)}, bf16[96,1152]{1,0:T(8,128)(2,1)S(1)}, u32[]{:S(2)}, u32[]{:S(2)}) collective-permute-start(bf16[96,1152]{1,0:T(8,128)(2,1)S(1)} %constant_dynamic-slice_fusion.28), channel_id=1, source_target_pairs={{0,1},{1,0},{2,3},{3,2},{4,5},{5,4},{6,7},{7,6},{8,9},{9,8},{10,11... | collective-permute-start | bytes 663560 | tf_op jit(solution)/shard_map/ppermute | solution.py:292
  407.7 21.8 %collective-permute-start.13 = (bf16[96,1152]{1,0:T(8,128)(2,1)S(1)}, bf16[96,1152]{1,0:T(8,128)(2,1)S(1)}, u32[]{:S(2)}, u32[]{:S(2)}) collective-permute-start(bf16[96,1152]{1,0:T(8,128)(2,1)S(1)} %constant_dynamic-slice_fusion.32), channel_id=1, source_target_pairs={{0,4},{1,5},{2,6},{3,7},{4,0},{5,1},{6,2},{7,3},{8,12},{9,13},{10,... | collective-permute-start | bytes 663560 | tf_op jit(solution)/shard_map/ppermute | solution.py:292
  416.0 8.8 %collective-permute-start.90 = (bf16[96,384]{1,0:T(8,128)(2,1)S(1)}, bf16[96,384]{1,0:T(8,128)(2,1)S(1)}, u32[]{:S(2)}, u32[]{:S(2)}) collective-permute-start(bf16[96,384]{1,0:T(8,128)(2,1)S(1)} %constant_dynamic-slice_fusion), channel_id=1, source_target_pairs={{0,16},{1,17},{2,18},{3,19},{4,20},{5,21},{6,22},{7,23},{8,24},{9,... | collective-permute-start | bytes 221192 | tf_op jit(solution)/shard_map/ppermute | solution.py:292
  416.7 9.7 %collective-permute-start.80 = (bf16[96,384]{1,0:T(8,128)(2,1)S(1)}, bf16[96,384]{1,0:T(8,128)(2,1)S(1)}, u32[]{:S(2)}, u32[]{:S(2)}) collective-permute-start(bf16[96,384]{1,0:T(8,128)(2,1)S(1)} %constant_dynamic-slice_fusion.4), channel_id=1, source_target_pairs={{0,16},{1,17},{2,18},{3,19},{4,20},{5,21},{6,22},{7,23},{8,24},{9,... | collective-permute-start | bytes 221192 | tf_op jit(solution)/shard_map/ppermute | solution.py:292
  419.8 13.2 %collective-permute-start.71 = (bf16[24,1536]{1,0:T(8,128)(2,1)S(1)}, bf16[24,1536]{1,0:T(8,128)(2,1)S(1)}, u32[]{:S(2)}, u32[]{:S(2)}) collective-permute-start(bf16[24,1536]{1,0:T(8,128)(2,1)S(1)} %add_convert_fusion.34), channel_id=1, source_target_pairs={{0,16},{1,17},{2,18},{3,19},{4,20},{5,21},{6,22},{7,23},{8,24},{9,... | collective-permute-start | bytes 221192 | tf_op jit(solution)/shard_map/ppermute | solution.py:292
  424.8 8.8 %collective-permute-start.61 = (bf16[24,1536]{1,0:T(8,128)(2,1)S(1)}, bf16[24,1536]{1,0:T(8,128)(2,1)S(1)}, u32[]{:S(2)}, u32[]{:S(2)}) collective-permute-start(bf16[24,1536]{1,0:T(8,128)(2,1)S(1)} %add_convert_fusion.35), channel_id=1, source_target_pairs={{0,16},{1,17},{2,18},{3,19},{4,20},{5,21},{6,22},{7,23},{8,24},{9,... | collective-permute-start | bytes 221192 | tf_op jit(solution)/shard_map/ppermute | solution.py:292
  426.4 9.5 %collective-permute-start.91 = (bf16[96,384]{1,0:T(8,128)(2,1)S(1)}, bf16[96,384]{1,0:T(8,128)(2,1)S(1)}, u32[]{:S(2)}, u32[]{:S(2)}) collective-permute-start(bf16[96,384]{1,0:T(8,128)(2,1)S(1)} %add_convert_fusion.32), channel_id=1, source_target_pairs={{0,16},{1,17},{2,18},{3,19},{4,20},{5,21},{6,22},{7,23},{8,24},{9,... | collective-permute-start | bytes 221192 | tf_op jit(solution)/shard_map/ppermute | solution.py:292
  427.8 9.5 %collective-permute-start.81 = (bf16[96,384]{1,0:T(8,128)(2,1)S(1)}, bf16[96,384]{1,0:T(8,128)(2,1)S(1)}, u32[]{:S(2)}, u32[]{:S(2)}) collective-permute-start(bf16[96,384]{1,0:T(8,128)(2,1)S(1)} %add_convert_fusion.33), channel_id=1, source_target_pairs={{0,16},{1,17},{2,18},{3,19},{4,20},{5,21},{6,22},{7,23},{8,24},{9,... | collective-permute-start | bytes 221192 | tf_op jit(solution)/shard_map/ppermute | solution.py:292
  429.5 9.4 %collective-permute-start.24 = (bf16[48,1152]{1,0:T(8,128)(2,1)S(1)}, bf16[48,1152]{1,0:T(8,128)(2,1)S(1)}, u32[]{:S(2)}, u32[]{:S(2)}) collective-permute-start(bf16[48,1152]{1,0:T(8,128)(2,1)S(1)} %constant_dynamic-slice_fusion.27), channel_id=1, source_target_pairs={{0,8},{1,9},{2,10},{3,11},{4,12},{5,13},{6,14},{7,15},{8,0},{9,1},... | collective-permute-start | bytes 331784 | tf_op jit(solution)/shard_map/ppermute | solution.py:292
  433.1 8.2 %collective-permute-start.14 = (bf16[48,1152]{1,0:T(8,128)(2,1)S(1)}, bf16[48,1152]{1,0:T(8,128)(2,1)S(1)}, u32[]{:S(2)}, u32[]{:S(2)}) collective-permute-start(bf16[48,1152]{1,0:T(8,128)(2,1)S(1)} %constant_dynamic-slice_fusion.31), channel_id=1, source_target_pairs={{0,8},{1,9},{2,10},{3,11},{4,12},{5,13},{6,14},{7,15},{8,0},{9,1},... | collective-permute-start | bytes 331784 | tf_op jit(solution)/shard_map/ppermute | solution.py:292
  433.6 24.9 %collective-permute-start.72 = (bf16[48,1536]{1,0:T(8,128)(2,1)S(1)}, bf16[48,1536]{1,0:T(8,128)(2,1)S(1)}, u32[]{:S(2)}, u32[]{:S(2)}) collective-permute-start(bf16[48,1536]{1,0:T(8,128)(2,1)S(1)} %pad_maximum_fusion.35), channel_id=1, source_target_pairs={{0,8},{1,9},{2,10},{3,11},{4,12},{5,13},{6,14},{7,15},{8,0},{9,1},... | collective-permute-start | bytes 442376 | tf_op jit(solution)/shard_map/ppermute | solution.py:292
  435.8 23.2 %collective-permute-start.62 = (bf16[48,1536]{1,0:T(8,128)(2,1)S(1)}, bf16[48,1536]{1,0:T(8,128)(2,1)S(1)}, u32[]{:S(2)}, u32[]{:S(2)}) collective-permute-start(bf16[48,1536]{1,0:T(8,128)(2,1)S(1)} %pad_maximum_fusion.34), channel_id=1, source_target_pairs={{0,8},{1,9},{2,10},{3,11},{4,12},{5,13},{6,14},{7,15},{8,0},{9,1},... | collective-permute-start | bytes 442376 | tf_op jit(solution)/shard_map/ppermute | solution.py:292
  437.3 22.7 %collective-permute-start.92 = (bf16[192,384]{1,0:T(8,128)(2,1)S(1)}, bf16[192,384]{1,0:T(8,128)(2,1)S(1)}, u32[]{:S(2)}, u32[]{:S(2)}) collective-permute-start(bf16[192,384]{1,0:T(8,128)(2,1)S(1)} %pad_maximum_fusion.37), channel_id=1, source_target_pairs={{0,8},{1,9},{2,10},{3,11},{4,12},{5,13},{6,14},{7,15},{8,0},{9,1},... | collective-permute-start | bytes 442376 | tf_op jit(solution)/shard_map/ppermute | solution.py:292
  438.8 22.0 %collective-permute-start.82 = (bf16[192,384]{1,0:T(8,128)(2,1)S(1)}, bf16[192,384]{1,0:T(8,128)(2,1)S(1)}, u32[]{:S(2)}, u32[]{:S(2)}) collective-permute-start(bf16[192,384]{1,0:T(8,128)(2,1)S(1)} %pad_maximum_fusion.36), channel_id=1, source_target_pairs={{0,8},{1,9},{2,10},{3,11},{4,12},{5,13},{6,14},{7,15},{8,0},{9,1},... | collective-permute-start | bytes 442376 | tf_op jit(solution)/shard_map/ppermute | solution.py:292
  441.2 8.1 %collective-permute-start.25 = (bf16[24,1152]{1,0:T(8,128)(2,1)S(1)}, bf16[24,1152]{1,0:T(8,128)(2,1)S(1)}, u32[]{:S(2)}, u32[]{:S(2)}) collective-permute-start(bf16[24,1152]{1,0:T(8,128)(2,1)S(1)} %constant_dynamic-slice_fusion.26), channel_id=1, source_target_pairs={{0,16},{1,17},{2,18},{3,19},{4,20},{5,21},{6,22},{7,23},{8,24},{9,... | collective-permute-start | bytes 165896 | tf_op jit(solution)/shard_map/ppermute | solution.py:292
  459.0 16.9 %collective-permute-start.73 = (bf16[96,1536]{1,0:T(8,128)(2,1)S(1)}, bf16[96,1536]{1,0:T(8,128)(2,1)S(1)}, u32[]{:S(2)}, u32[]{:S(2)}) collective-permute-start(bf16[96,1536]{1,0:T(8,128)(2,1)S(1)} %pad_maximum_fusion.27), channel_id=1, source_target_pairs={{0,1},{1,0},{2,3},{3,2},{4,5},{5,4},{6,7},{7,6},{8,9},{9,8},{10,11... | collective-permute-start | bytes 884744 | tf_op jit(solution)/shard_map/ppermute | solution.py:292
  460.0 17.0 %collective-permute-start.63 = (bf16[96,1536]{1,0:T(8,128)(2,1)S(1)}, bf16[96,1536]{1,0:T(8,128)(2,1)S(1)}, u32[]{:S(2)}, u32[]{:S(2)}) collective-permute-start(bf16[96,1536]{1,0:T(8,128)(2,1)S(1)} %pad_maximum_fusion.26), channel_id=1, source_target_pairs={{0,4},{1,5},{2,6},{3,7},{4,0},{5,1},{6,2},{7,3},{8,12},{9,13},{10,... | collective-permute-start | bytes 884744 | tf_op jit(solution)/shard_map/ppermute | solution.py:292
  460.8 17.8 %collective-permute-start.93 = (bf16[384,384]{1,0:T(8,128)(2,1)S(1)}, bf16[384,384]{1,0:T(8,128)(2,1)S(1)}, u32[]{:S(2)}, u32[]{:S(2)}) collective-permute-start(bf16[384,384]{1,0:T(8,128)(2,1)S(1)} %pad_maximum_fusion.29), channel_id=1, source_target_pairs={{0,1},{1,0},{2,3},{3,2},{4,5},{5,4},{6,7},{7,6},{8,9},{9,8},{10,11... | collective-permute-start | bytes 884744 | tf_op jit(solution)/shard_map/ppermute | solution.py:292
  463.0 17.3 %collective-permute-start.83 = (bf16[384,384]{1,0:T(8,128)(2,1)S(1)}, bf16[384,384]{1,0:T(8,128)(2,1)S(1)}, u32[]{:S(2)}, u32[]{:S(2)}) collective-permute-start(bf16[384,384]{1,0:T(8,128)(2,1)S(1)} %pad_maximum_fusion.28), channel_id=1, source_target_pairs={{0,4},{1,5},{2,6},{3,7},{4,0},{5,1},{6,2},{7,3},{8,12},{9,13},{10,... | collective-permute-start | bytes 884744 | tf_op jit(solution)/shard_map/ppermute | solution.py:292
  475.2 8.3 %collective-permute-start.28 = (bf16[96,1152]{1,0:T(8,128)(2,1)S(1)}, bf16[96,1152]{1,0:T(8,128)(2,1)S(1)}, u32[]{:S(2)}, u32[]{:S(2)}) collective-permute-start(bf16[96,1152]{1,0:T(8,128)(2,1)S(1)} %pad_maximum_fusion.31), channel_id=1, source_target_pairs={{0,1},{1,0},{2,3},{3,2},{4,5},{5,4},{6,7},{7,6},{8,9},{9,8},{10,11... | collective-permute-start | bytes 663560 | tf_op jit(solution)/shard_map/ppermute | solution.py:292
  475.9 8.4 %collective-permute-start.18 = (bf16[96,1152]{1,0:T(8,128)(2,1)S(1)}, bf16[96,1152]{1,0:T(8,128)(2,1)S(1)}, u32[]{:S(2)}, u32[]{:S(2)}) collective-permute-start(bf16[96,1152]{1,0:T(8,128)(2,1)S(1)} %pad_maximum_fusion.30), channel_id=1, source_target_pairs={{0,4},{1,5},{2,6},{3,7},{4,0},{5,1},{6,2},{7,3},{8,12},{9,13},{10,... | collective-permute-start | bytes 663560 | tf_op jit(solution)/shard_map/ppermute | solution.py:292
  477.1 41.7 %collective-permute-start.74 = (bf16[192,1536]{1,0:T(8,128)(2,1)S(1)}, bf16[192,1536]{1,0:T(8,128)(2,1)S(1)}, u32[]{:S(2)}, u32[]{:S(2)}) collective-permute-start(bf16[192,1536]{1,0:T(8,128)(2,1)S(1)} %pad_maximum_fusion.11), channel_id=1, source_target_pairs={{0,4},{1,5},{2,6},{3,7},{4,0},{5,1},{6,2},{7,3},{8,12},{9,13},{10,... | collective-permute-start | bytes 1769480 | tf_op jit(solution)/shard_map/ppermute | solution.py:292
  478.6 41.0 %collective-permute-start.64 = (bf16[192,1536]{1,0:T(8,128)(2,1)S(1)}, bf16[192,1536]{1,0:T(8,128)(2,1)S(1)}, u32[]{:S(2)}, u32[]{:S(2)}) collective-permute-start(bf16[192,1536]{1,0:T(8,128)(2,1)S(1)} %pad_maximum_fusion.10), channel_id=1, source_target_pairs={{0,1},{1,0},{2,3},{3,2},{4,5},{5,4},{6,7},{7,6},{8,9},{9,8},{10,11... | collective-permute-start | bytes 1769480 | tf_op jit(solution)/shard_map/ppermute | solution.py:292
  480.3 39.7 %collective-permute-start.94 = (bf16[768,384]{1,0:T(8,128)(2,1)S(1)}, bf16[768,384]{1,0:T(8,128)(2,1)S(1)}, u32[]{:S(2)}, u32[]{:S(2)}) collective-permute-start(bf16[768,384]{1,0:T(8,128)(2,1)S(1)} %pad_maximum_fusion.13), channel_id=1, source_target_pairs={{0,4},{1,5},{2,6},{3,7},{4,0},{5,1},{6,2},{7,3},{8,12},{9,13},{10,... | collective-permute-start | bytes 1769480 | tf_op jit(solution)/shard_map/ppermute | solution.py:292
  483.5 37.4 %collective-permute-start.84 = (bf16[768,384]{1,0:T(8,128)(2,1)S(1)}, bf16[768,384]{1,0:T(8,128)(2,1)S(1)}, u32[]{:S(2)}, u32[]{:S(2)}) collective-permute-start(bf16[768,384]{1,0:T(8,128)(2,1)S(1)} %pad_maximum_fusion.12), channel_id=1, source_target_pairs={{0,1},{1,0},{2,3},{3,2},{4,5},{5,4},{6,7},{7,6},{8,9},{9,8},{10,11... | collective-permute-start | bytes 1769480 | tf_op jit(solution)/shard_map/ppermute | solution.py:292
  484.3 25.9 %collective-permute-start.29 = (bf16[192,1152]{1,0:T(8,128)(2,1)S(1)}, bf16[192,1152]{1,0:T(8,128)(2,1)S(1)}, u32[]{:S(2)}, u32[]{:S(2)}) collective-permute-start(bf16[192,1152]{1,0:T(8,128)(2,1)S(1)} %pad_maximum_fusion.23), channel_id=1, source_target_pairs={{0,4},{1,5},{2,6},{3,7},{4,0},{5,1},{6,2},{7,3},{8,12},{9,13},{10,... | collective-permute-start | bytes 1327112 | tf_op jit(solution)/shard_map/ppermute | solution.py:292
  510.2 8.3 %collective-permute-start.19 = (bf16[192,1152]{1,0:T(8,128)(2,1)S(1)}, bf16[192,1152]{1,0:T(8,128)(2,1)S(1)}, u32[]{:S(2)}, u32[]{:S(2)}) collective-permute-start(bf16[192,1152]{1,0:T(8,128)(2,1)S(1)} %pad_maximum_fusion.22), channel_id=1, source_target_pairs={{0,1},{1,0},{2,3},{3,2},{4,5},{5,4},{6,7},{7,6},{8,9},{9,8},{10,11... | collective-permute-start | bytes 1327112 | tf_op jit(solution)/shard_map/ppermute | solution.py:292
  519.6 18.7 %collective-permute-start.75 = (bf16[384,1536]{1,0:T(8,128)(2,1)S(1)}, bf16[384,1536]{1,0:T(8,128)(2,1)S(1)}, u32[]{:S(2)}, u32[]{:S(2)}) collective-permute-start(bf16[384,1536]{1,0:T(8,128)(2,1)S(1)} %pad_maximum_fusion.5), channel_id=1, source_target_pairs={{0,2},{1,3},{2,0},{3,1},{4,6},{5,7},{6,4},{7,5},{8,10},{9,11},{10,... | collective-permute-start | bytes 3538952 | tf_op jit(solution)/shard_map/ppermute | solution.py:292
  520.0 18.7 %collective-permute-start.65 = (bf16[384,1536]{1,0:T(8,128)(2,1)S(1)}, bf16[384,1536]{1,0:T(8,128)(2,1)S(1)}, u32[]{:S(2)}, u32[]{:S(2)}) collective-permute-start(bf16[384,1536]{1,0:T(8,128)(2,1)S(1)} %pad_maximum_fusion.4), channel_id=1, source_target_pairs={{0,2},{1,3},{2,0},{3,1},{4,6},{5,7},{6,4},{7,5},{8,10},{9,11},{10,... | collective-permute-start | bytes 3538952 | tf_op jit(solution)/shard_map/ppermute | solution.py:292
  520.9 18.2 %collective-permute-start.95 = (bf16[1536,384]{1,0:T(8,128)(2,1)S(1)}, bf16[1536,384]{1,0:T(8,128)(2,1)S(1)}, u32[]{:S(2)}, u32[]{:S(2)}) collective-permute-start(bf16[1536,384]{1,0:T(8,128)(2,1)S(1)} %pad_maximum_fusion.7), channel_id=1, source_target_pairs={{0,2},{1,3},{2,0},{3,1},{4,6},{5,7},{6,4},{7,5},{8,10},{9,11},{10,... | collective-permute-start | bytes 3538952 | tf_op jit(solution)/shard_map/ppermute | solution.py:292
  521.4 39.6 %collective-permute-start.85 = (bf16[1536,384]{1,0:T(8,128)(2,1)S(1)}, bf16[1536,384]{1,0:T(8,128)(2,1)S(1)}, u32[]{:S(2)}, u32[]{:S(2)}) collective-permute-start(bf16[1536,384]{1,0:T(8,128)(2,1)S(1)} %pad_maximum_fusion.6), channel_id=1, source_target_pairs={{0,2},{1,3},{2,0},{3,1},{4,6},{5,7},{6,4},{7,5},{8,10},{9,11},{10,... | collective-permute-start | bytes 3538952 | tf_op jit(solution)/shard_map/ppermute | solution.py:292
  (92 other events, 790.8 us)
